TPU v7x, 128 devices: a whole 4x4x4 slice. The times are simulated.
128 devices in a mesh: table: 32 (over z, x, core), sub: 4 (over y).
Axes of the slice: x: 4, y: 4, z: 4, core: 2. Of those that a mesh axis runs over, the one named last changes fastest.
Arguments:
- pooled: bfloat16 [96, 32, 4, 32, 128], P('table', None, 'sub'), may hold values from -6 to 6
- field_owner: int32 [48], replicated, may hold values from 0 to 31, as said below
- w_squeeze: float32 [16, 48], replicated, may hold values from -2.5 to 2.5
- w_excite: float32 [1536, 16], replicated, may hold values from -1.5 to 1.5
- w_bilinear: float32 [32, 32], replicated, may hold values from -1 to 1
- tower_weight: bfloat16 [36096, 1024], P(('table', 'sub')), may hold values from -0.1875 to 0.1875
- tower_cotangent: bfloat16 [1024, 16384], P(None, ('table', 'sub')), may hold values from -6 to 6
Outputs:
- row_grads: bfloat16 [96, 32, 4, 32, 128], P('table', None, 'sub')
- tower_weight_grad: float32 [36096, 1024], P(('table', 'sub'))
- squeeze_grad: float32 [16, 48], replicated
- excite_grad: float32 [1536, 16], replicated
- bilinear_grad: float32 [32, 32], replicated
Inputs may be any that keep to these rules, and one draw needn't show every extreme that they name: `field_owner`: each table index holds at most 3 fields, and some index holds exactly 3.
All inputs are finite; a program needn't handle non-finite values.
Results may differ from a plain program's by a relative error of at most 0.0074.
Values may be sent and summed in bfloat16 or wider, within the bound.
No kernel may reach another device: no remote copies, remote signals or barrier semaphores. Data moves between devices by JAX's collectives and lax.ppermute only.
A program may use at most 192 MiB of HBM per device.

v0:
```python
import functools

import jax
import jax.numpy as jnp
import numpy as np
from jax import lax
from jax.experimental import pallas as pl
from jax.experimental.pallas import tpu as pltpu
from jax.sharding import PartitionSpec as P


HIGH = lax.Precision.HIGHEST
BOTH = ("table", "sub")
PLANES = 4
LIMIT = 13

WORKER = (
    4, 3, 2, 5, 0, 2, 4, 3, 7, 3, 0, 4, 6, 2, 2, 6, 6, 3, 4, 0, 3, 7, 1, 1, 5, 7, 6, 0, 5, 6, 7, 1, 2, 1, 5, 5, 1, 4, 3, 2, 2, 4, 7, 7, 0, 1, 5,
    5, 0, 6, 1, 6, 4, 3, 7, 3, 0, 4, 6, 2, 2, 1, 6, 3, 4, 0, 3, 0, 2, 1, 6, 7, 6, 0, 5, 6, 7, 1, 2, 1, 5, 5, 1, 4, 3, 2, 2, 4, 7, 7, 0, 1, 5, 1,
    5, 4, 3, 4, 3, 7, 3, 0, 4, 6, 2, 2, 6, 6, 3, 4, 0, 3, 7, 2, 1, 6, 7, 6, 0, 5, 6, 7, 1, 2, 1, 5, 5, 1, 4, 3, 2, 2, 4, 5, 7, 0, 1, 5, 7, 3, 4,
    4, 3, 7, 3, 0, 4, 6, 2, 2, 6, 6, 3, 4, 0, 3, 0, 1, 1, 5, 7, 6, 0, 5, 6, 7, 1, 2, 1, 5, 5, 1, 4, 3, 2, 2, 4, 5, 7, 0, 5, 5, 1, 7, 4, 3, 7, 3,
    0, 4, 6, 2, 2, 6, 6, 3, 4, 0, 3, 0, 2, 1, 5, 7, 6, 0, 5, 6, 7, 1, 2, 1, 5, 5, 1, 4, 3, 2, 2, 4, 5, 7, 0, 5, 5, 0, 4, 3, 7, 3, 0, 4, 6, 2, 2,
    6, 6, 3, 4, 0, 3, 7, 2, 1, 6, 7, 6, 0, 5, 6, 7, 1, 2, 1, 5, 5, 1, 4, 3, 2, 2, 4, 7, 7, 0, 5, 5, 4, 3, 7, 3, 0, 4, 6, 2, 2, 6, 6, 3, 4, 0, 3,
    1, 5, 7, 6, 6, 4, 0, 1, 5, 2, 1, 4, 7, 0, 6, 0, 6, 3, 4, 7, 1, 7, 3, 0, 3, 5, 6, 0, 2, 3, 2, 4, 3, 2, 4, 1, 5, 3, 2, 2, 1, 5, 7, 6, 6, 4, 0,
    1, 5, 2, 1, 4, 7, 0, 6, 0, 6, 3, 4, 7, 1, 7, 3, 0, 3, 5, 7, 4, 3, 6, 5, 3, 2, 4, 1, 5, 3, 2, 2, 1, 5, 7, 6, 6, 4, 2, 1, 5, 2, 1, 4, 7, 0, 6,
    0, 6, 3, 4, 7, 1, 7, 6, 0, 3, 5, 7, 0, 3, 5, 3, 2, 4, 1, 5, 3, 2, 2, 1, 5, 7, 0, 6, 4, 2, 1, 5, 2, 1, 4, 7, 0, 6, 0, 6, 3, 4, 7, 1, 7, 3, 0,
    3, 5, 3, 7, 5, 3, 2, 4, 1, 5, 3, 2, 2, 1, 5, 7, 0, 6, 4, 2, 1, 5, 2, 1, 4, 7, 0, 6, 0, 6, 3, 4, 7, 1, 7, 6, 0, 3, 5, 5, 4, 3, 2, 4, 1, 5, 3,
    2, 2, 1, 5, 7, 0, 6, 4, 0, 1, 5, 2, 1, 4, 7, 0, 6, 0, 6, 3, 4, 7, 1, 7, 3, 0, 3, 5, 2, 3, 2, 4, 1, 5, 3, 2, 2, 1, 5, 7, 0, 6, 4, 0, 1, 5, 2,
    1, 4, 7, 0, 6, 0, 6, 3, 4, 7, 1, 7, 6, 0, 3, 5, 3, 2, 4, 1, 5, 3, 2, 2, 1, 5, 7, 0, 6, 4, 2, 1, 5, 2, 1, 4, 7, 0, 6, 0, 6, 3, 4, 7, 1, 7, 6,
    0, 0, 0, 4, 2, 7, 7, 3, 5, 6, 4, 2, 5, 1, 3, 6, 1, 6, 7, 3, 4, 3, 1, 1, 4, 5, 7, 6, 1, 2, 4, 5, 7, 5, 2, 2, 4, 0, 0, 2, 0, 6, 1, 3, 5, 1, 3,
    6, 1, 6, 7, 3, 4, 3, 1, 5, 4, 5, 7, 6, 2, 0, 4, 1, 7, 5, 0, 2, 4, 3, 7, 3, 1, 1, 6, 0, 1, 3, 6, 2, 6, 7, 3, 4, 3, 2, 1, 4, 0, 7, 6, 2, 0, 4,
    1, 7, 0, 2, 2, 0, 7, 3, 4, 4, 6, 5, 5, 3, 6, 2, 6, 7, 3, 4, 3, 2, 5, 4, 0, 7, 6, 2, 0, 4, 5, 7, 5, 2, 0, 7, 0, 1, 4, 4, 0, 1, 3, 6, 1, 6, 7,
    3, 4, 3, 1, 1, 4, 0, 7, 6, 1, 0, 4, 1, 7, 0, 0, 0, 6, 2, 7, 2, 5, 5, 3, 6, 2, 6, 7, 3, 4, 3, 2, 5, 4, 5, 7, 6, 2, 2, 4, 5, 7, 5, 2, 2, 3, 0,
    6, 5, 1, 3, 6, 1, 6, 7, 3, 4, 3, 1, 1, 4, 0, 7, 6, 1, 0, 4, 5, 7, 0, 0, 0, 3, 4, 5, 1, 3, 6, 2, 6, 7, 3, 4, 3, 1, 5, 4, 5, 7, 6, 2, 2, 4, 5,
    7, 5, 2, 2, 7, 0, 1, 3, 6, 1, 6, 7, 3, 4, 3, 1, 1, 4, 0, 7, 6, 1, 0, 4, 1, 7, 0, 0, 0, 5, 5, 3, 6, 2, 6, 7, 3, 4, 3, 2, 5, 4, 5, 7, 6, 2, 2,
    6, 6, 6, 1, 1, 1, 3, 5, 7, 5, 7, 0, 7, 0, 5, 0, 2, 3, 0, 5, 2, 0, 2, 5, 7, 3, 2, 7, 3, 3, 4, 2, 4, 1, 1, 4, 1, 3, 2, 3, 4, 2, 2, 4, 2, 4, 4,
    3, 2, 1, 1, 0, 6, 7, 5, 0, 0, 7, 3, 6, 6, 7, 5, 0, 5, 6, 7, 5, 6, 3, 7, 3, 6, 4, 6, 7, 3, 7, 0, 6, 7, 4, 3, 3, 0, 0, 4, 6, 4, 4, 7, 3, 1, 1,
    5, 2, 1, 2, 6, 1, 5, 2, 2, 1, 2, 5, 5, 6, 2, 6, 5, 1, 7, 4, 1, 4, 2, 7, 4, 2, 7, 1, 2, 4, 2, 7, 4, 7, 1, 5, 3, 0, 3, 6, 3, 0, 3, 0, 1, 6, 5,
    6, 6, 1, 6, 6, 5, 7, 4, 4, 1, 7, 5, 0, 1, 0, 7, 5, 7, 4, 7, 1, 5, 0, 2, 3, 5, 2, 3, 4, 0, 4, 2, 0, 3, 2, 3, 0, 1, 7, 5, 5, 7, 5, 0, 5, 5, 7,
    1, 1, 1, 2, 3, 4, 3, 0, 4, 0, 4, 4, 0, 3, 2, 3, 6, 4, 2, 2, 1, 6, 6, 6, 4, 2, 1, 1, 7, 3, 3, 1, 6, 6, 6, 3, 1, 6, 1, 5, 7, 0, 0, 4, 4, 4, 4,
    7, 5, 3, 5, 2, 5, 2, 3, 2, 2, 5, 0, 0, 7, 2, 3, 2, 2, 3, 0, 4, 5, 0, 1, 1, 5, 6, 6, 0, 2, 2, 6, 5, 6, 4, 7, 5, 7, 4, 7, 5, 3, 7, 3, 1, 1, 6,
)


@functools.lru_cache(maxsize=None)
def make_plan(count, tables, subs, width, rows):
    plane = tables // PLANES
    held = rows * subs
    unit = 8
    assert width % unit == 0 and held % unit == 0
    pairs = [(i, j) for i in range(count) for j in range(i + 1, count)]
    assert len(pairs) == len(WORKER) and len(pairs) * width == held * tables
    per_plane = len(pairs) // PLANES
    worker = [plane * (g // per_plane) + WORKER[g] for g in range(len(pairs))]
    fields = [set() for _ in range(tables)]
    for g, r in enumerate(worker):
        fields[r] |= set(pairs[g])
    fields = [sorted(s) for s in fields]
    assert max(len(s) for s in fields) <= LIMIT
    table = np.zeros((tables, LIMIT), np.int32)
    live = np.zeros((tables, LIMIT), bool)
    for r, s in enumerate(fields):
        table[r, : len(s)] = s
        live[r, : len(s)] = True
    touched = [[[] for _ in range(plane)] for _ in range(tables)]
    for t in range(tables):
        for g in range(held * t // width, (held * (t + 1) - 1) // width + 1):
            assert worker[g] // plane == t // plane
            touched[t][worker[g] % plane].append(g)
    depth = max(len(x) for y in touched for x in y)
    units = held // unit
    per = width // unit
    pick = np.full((tables, plane, depth, per), units, np.int32)
    back = np.zeros((tables, units), np.int32)
    left = np.zeros((tables, plane * depth), np.int32)
    right = np.zeros((tables, plane * depth), np.int32)
    for t in range(tables):
        for w in range(plane):
            for c, g in enumerate(touched[t][w]):
                r = t // plane * plane + w
                k = (t % plane) ^ w
                slot = k * depth + c
                left[r, slot] = fields[r].index(pairs[g][0])
                right[r, slot] = fields[r].index(pairs[g][1])
                for q in range(per):
                    u = (width * g - held * t) // unit + q
                    if 0 <= u < units:
                        pick[t, k, c, q] = u
                        back[t, u] = (k * depth + c) * per + q
    return dict(
        table=table, live=live, depth=depth, pick=pick.reshape(tables, -1), back=back,
        left=left, right=right, plane=plane, unit=unit, units=units,
    )


def hadamard_np(width):
    index = np.arange(width)
    both = index[:, None] & index[None, :]
    parity = np.zeros((width, width), int)
    for bit_pos in range(width.bit_length()):
        parity = parity ^ (both >> bit_pos & 1)
    return (1 - 2 * parity).astype(np.float32)


def slot_table(field_owner, per_owner):
    count = field_owner.shape[0]
    order = jnp.arange(count, dtype=jnp.int32)
    same = field_owner[:, None] == field_owner[None, :]
    earlier = order[:, None] > order[None, :]
    position = jnp.sum((same & earlier).astype(jnp.int32), axis=1)
    return field_owner * per_owner + position


def swap(value, axis, size, k):
    return lax.ppermute(value, axis, [(a, a ^ k) for a in range(size)])


def trade(blocks, axis, size):
    return [blocks[0]] + [swap(b, axis, size, k) for k, b in enumerate(blocks) if k]


def xor_order(blocks, axis):
    own = lax.axis_index(axis)
    return jnp.take(blocks, own ^ jnp.arange(blocks.shape[0], dtype=jnp.int32), axis=0, mode="clip")


def halves(x):
    high = x.astype(jnp.bfloat16)
    return high, (x - high.astype(jnp.float32)).astype(jnp.bfloat16)


def pack_rows(received, squeezed, slot_index, table):
    slots, width, samples = received.shape
    count = squeezed.shape[0]
    tables = table.shape[0] // LIMIT
    total = LIMIT * width + count
    turn = 8

    def body(slot_ref, table_ref, received_ref, squeezed_ref, out_ref):
        first = pl.program_id(0) * (turn * LIMIT)
        for r in range(turn):
            for k in range(LIMIT):
                out_ref[r, k * width : (k + 1) * width, :] = received_ref[
                    slot_ref[table_ref[first + r * LIMIT + k]]
                ]
            out_ref[r, LIMIT * width :, :] = squeezed_ref[...]

    return pl.pallas_call(
        body,
        out_shape=jax.ShapeDtypeStruct((tables, total, samples), received.dtype),
        grid_spec=pltpu.PrefetchScalarGridSpec(
            num_scalar_prefetch=2,
            grid=(tables // turn,),
            in_specs=[
                pl.BlockSpec((slots, width, samples), lambda i, *_: (0, 0, 0)),
                pl.BlockSpec((count, samples), lambda i, *_: (0, 0)),
            ],
            out_specs=pl.BlockSpec((turn, total, samples), lambda i, *_: (i, 0, 0)),
        ),
        name="pack_rows",
    )(slot_index, table, received, squeezed)


def tower_pairs(own, pieces, cotangent):
    tall, quarter = pieces[0].shape
    hidden, cols = cotangent.shape
    parts = len(pieces)
    step = 512

    def body(own_ref, *refs):
        cot_ref, out_ref, rows_ref = refs[parts:]

        @pl.when(pl.program_id(0) == 0)
        def _():
            for o in range(parts):

                @pl.when(own_ref[0] == o)
                def _(o=o):
                    for q in range(parts):
                        rows_ref[:, q * quarter : (q + 1) * quarter] = refs[o ^ q][...]

        out_ref[...] = jnp.dot(
            rows_ref[...], cot_ref[...], preferred_element_type=jnp.float32
        ).astype(out_ref.dtype)

    return pl.pallas_call(
        body,
        out_shape=jax.ShapeDtypeStruct((tall, cols), cotangent.dtype),
        grid_spec=pltpu.PrefetchScalarGridSpec(
            num_scalar_prefetch=1,
            grid=(cols // step,),
            in_specs=[
                *[pl.BlockSpec((tall, quarter), lambda i, *_: (0, 0)) for _ in pieces],
                pl.BlockSpec((hidden, step), lambda i, *_: (0, i)),
            ],
            out_specs=pl.BlockSpec((tall, step), lambda i, *_: (0, i)),
            scratch_shapes=[pltpu.VMEM((tall, hidden), cotangent.dtype)],
        ),
        compiler_params=pltpu.CompilerParams(vmem_limit_bytes=40 * 1024 * 1024),
        cost_estimate=pl.CostEstimate(
            flops=2 * tall * hidden * cols, transcendentals=0, bytes_accessed=30_000_000
        ),
        name="tower_pairs",
    )(own, *pieces, cotangent)


def owner_step(parts, selected, squeezed, table, slot_index, w_ex, w_ext, w_sq, w_sqt, slots):
    tables, span, samples = parts.shape
    count, width, _ = selected.shape
    scale = 1.0 / width**0.5
    f32, bf16 = jnp.float32, jnp.bfloat16
    turn = 8
    bundle = 8

    def dot(a, b):
        return jnp.dot(a, b, preferred_element_type=f32)

    def body(table_ref, slot_ref, parts_ref, sel_ref, sq_ref, hd_ref, wex_ref, wext_ref, wsq_ref,
             wsqt_ref, out_ref, acc, ex, sp):
        step = pl.program_id(0)

        @pl.when(step == 0)
        def _():
            acc[...] = jnp.zeros_like(acc)

        for r in range(turn):
            for k in range(LIMIT):
                f = table_ref[(step * turn + r) * LIMIT + k]
                acc[f] += parts_ref[r, k * width : (k + 1) * width, :].astype(f32)

        @pl.when(step == pl.num_programs(0) - 1)
        def _():
            sq = sq_ref[...]
            pre = dot(wsq_ref[...], jnp.concatenate([sq, sq, sq], axis=0)) * scale
            gate = 1.0 / (1.0 + jnp.exp(-pre))
            ah, al = halves(pre * gate)
            ex[...] = dot(wex_ref[...], jnp.concatenate([ah, ah, al], axis=0))
            d_act = jnp.zeros(pre.shape, f32)
            for b in range(count // bundle):
                at = slice(b * bundle * width, (b + 1) * bundle * width)
                rows = sel_ref[b * bundle : (b + 1) * bundle].reshape(bundle * width, samples)
                fields = dot(hd_ref[...], rows) * scale
                got = acc[b * bundle : (b + 1) * bundle].reshape(bundle * width, samples)
                eh, el = halves(got * fields)
                d_act = d_act + dot(wext_ref[b, 0], eh) + dot(wext_ref[b, 0], el)
                d_act = d_act + dot(wext_ref[b, 1], eh)
                ex[at] = got * (1.0 + ex[at])
            d_pre = d_act * gate * (1.0 + pre * (1.0 - gate))
            ph, pl_ = halves(d_pre)
            sp[...] = dot(wsqt_ref[...], jnp.concatenate([ph, pl_, ph], axis=0)) * (1.0 / width)
            out_ref[...] = jnp.zeros_like(out_ref)
            for f in range(count):
                grad = ex[f * width : (f + 1) * width] + sp[f : f + 1, :]
                out_ref[slot_ref[f]] = grad.astype(bf16)

    hd = jnp.asarray(np.kron(np.eye(bundle), hadamard_np(width)), bf16)
    mats = (selected, squeezed, hd, w_ex, w_ext, w_sq, w_sqt)
    return pl.pallas_call(
        body,
        out_shape=jax.ShapeDtypeStruct((slots, width, samples), bf16),
        grid_spec=pltpu.PrefetchScalarGridSpec(
            num_scalar_prefetch=2,
            grid=(tables // turn,),
            in_specs=[
                pl.BlockSpec((turn, span, samples), lambda i, *_: (i, 0, 0)),
                *[pl.BlockSpec(m.shape, lambda i, *_, n=m.ndim: (0,) * n) for m in mats],
            ],
            out_specs=pl.BlockSpec((slots, width, samples), lambda i, *_: (0, 0, 0)),
            scratch_shapes=[
                pltpu.VMEM((count, width, samples), f32),
                pltpu.VMEM((count * width, samples), f32),
                pltpu.VMEM((count, samples), f32),
            ],
        ),
        compiler_params=pltpu.CompilerParams(vmem_limit_bytes=40 * 1024 * 1024),
        name="owner_step",
    )(table, slot_index, parts, *mats)


def pair_step(got, pair_grad, left, right, signs, w_pairs, w_ex, w_ext, w_sq, width):
    tables, tall, samples = got.shape
    slots = left.shape[0]
    units = w_sq.shape[0]
    count = tall - LIMIT * width
    span = LIMIT * width
    group = 4
    cols = group * samples
    scale = 1.0 / width**0.5
    f32, bf16 = jnp.float32, jnp.bfloat16

    def dot(a, b):
        return jnp.dot(a, b, preferred_element_type=f32)

    def dot_nt(a, b):
        return lax.dot_general(a, b, (((1,), (1,)), ((), ())), preferred_element_type=f32)

    half = (LIMIT + 1) // 2 * width
    spans = [slice(0, half), slice(half, span)]

    def blocks(a, b):
        return jnp.concatenate([dot(a[s, : s.stop - s.start], b[s]) for s in spans], axis=0)

    def body(left_ref, right_ref, got_ref, pg_ref, hd_ref, rep_ref, rept_ref, mask_ref, wb_ref,
             wex_ref, wext_ref, wsq_ref, pairs_ref, part_ref, dbil_ref, dex_ref, dsq_ref,
             wt, mp, dm, dw, mats):
        @pl.when(pl.program_id(0) == 0)
        def _():
            for k in range(4):
                tall = dot(rep_ref[...], wb_ref[k]).astype(bf16)
                mats[k] = (dot(tall, rept_ref[...]) * mask_ref[...]).astype(bf16)
            dbil_ref[...] = jnp.zeros_like(dbil_ref)
            dex_ref[...] = jnp.zeros_like(dex_ref)
            dsq_ref[...] = jnp.zeros_like(dsq_ref)

        rows = jnp.concatenate([got_ref[o] for o in range(group)], axis=1)
        sq = rows[span:]
        fields = blocks(hd_ref, rows[:span]) * scale
        pre = dot(wsq_ref[...], jnp.concatenate([sq, sq, sq], axis=0)) * scale
        gate = 1.0 / (1.0 + jnp.exp(-pre))
        act = pre * gate
        ah, al = halves(act)
        excite = dot(wex_ref[...], jnp.concatenate([ah, ah, al], axis=0))
        weighted = fields * (1.0 + excite)
        wh, wl = halves(weighted)
        mapped = blocks(mats.at[0], wh) + blocks(mats.at[0], wl) + blocks(mats.at[1], wh)
        wt[...] = weighted.reshape(LIMIT, width, cols)
        mp[...] = mapped.reshape(LIMIT, width, cols)
        dm[...] = jnp.zeros_like(dm)
        dw[...] = jnp.zeros_like(dw)

        def one(p, carry):
            i = left_ref[p]
            j = right_ref[p]
            off = pl.multiple_of(p * width, width)
            x = mp[i]
            y = wt[j]
            pairs_ref[pl.ds(off, width), :] = (x * y).astype(bf16)
            g = pg_ref[pl.ds(off, width), :].astype(f32)
            dm[i] += g * y
            dw[j] += g * x
            return carry

        lax.fori_loop(0, slots, one, 0, unroll=2)
        dmv = dm[...].reshape(span, cols)
        dh, dl = halves(dmv)
        part = dw[...].reshape(span, cols) + (
            blocks(mats.at[2], dh) + blocks(mats.at[2], dl) + blocks(mats.at[3], dh)
        )
        sent = part.astype(bf16)
        for o in range(group):
            part_ref[o] = sent[:, o * samples : (o + 1) * samples]
        d_excite = part * fields
        eh, el = halves(d_excite)
        d_act = dot(wext_ref[...], jnp.concatenate([eh, el, eh], axis=0))
        d_pre = d_act * gate * (1.0 + pre * (1.0 - gate))
        ph, pl_ = halves(d_pre)

        for s in spans:
            dbil_ref[s, : s.stop - s.start] += dot_nt(wh[s], dh[s])
        dex_ref[...] += dot_nt(jnp.concatenate([ah, al], axis=0), eh)
        dsq_ref[...] += dot_nt(jnp.concatenate([ph, pl_], axis=0), sq)

    def whole(a):
        return pl.BlockSpec(a.shape, lambda i, *_, n=a.ndim: (0,) * n)

    block = np.kron(np.eye(LIMIT), np.ones((width, width)))
    turned = np.zeros((span, half), np.float32)
    mask = np.zeros((span, half), np.float32)
    for s in spans:
        turned[s, : s.stop - s.start] = np.kron(np.eye(LIMIT), signs)[s, s]
        mask[s, : s.stop - s.start] = block[s, s]
    repeat = np.tile(np.eye(width), (LIMIT, 1))
    mats = (
        jnp.asarray(turned, bf16),
        jnp.asarray(repeat, bf16),
        jnp.asarray(repeat[:half].T, bf16),
        jnp.asarray(mask, f32),
        w_pairs,
        w_ex,
        w_ext,
        w_sq,
    )
    return pl.pallas_call(
        body,
        out_shape=(
            jax.ShapeDtypeStruct((slots * width, tables * samples), bf16),
            jax.ShapeDtypeStruct((tables, span, samples), bf16),
            jax.ShapeDtypeStruct((span, half), f32),
            jax.ShapeDtypeStruct((2 * units, span), f32),
            jax.ShapeDtypeStruct((2 * units, count), f32),
        ),
        grid_spec=pltpu.PrefetchScalarGridSpec(
            num_scalar_prefetch=2,
            grid=(tables // group,),
            in_specs=[
                pl.BlockSpec((group, got.shape[1], samples), lambda i, *_: (i, 0, 0)),
                pl.BlockSpec((slots * width, cols), lambda i, *_: (0, i)),
                *[whole(m) for m in mats],
            ],
            out_specs=[
                pl.BlockSpec((slots * width, cols), lambda i, *_: (0, i)),
                pl.BlockSpec((group, span, samples), lambda i, *_: (i, 0, 0)),
                pl.BlockSpec((span, half), lambda i, *_: (0, 0)),
                pl.BlockSpec((2 * units, span), lambda i, *_: (0, 0)),
                pl.BlockSpec((2 * units, count), lambda i, *_: (0, 0)),
            ],
            scratch_shapes=[
                *[pltpu.VMEM((LIMIT, width, cols), f32) for _ in range(4)],
                pltpu.VMEM((4, span, half), bf16),
            ],
        ),
        compiler_params=pltpu.CompilerParams(vmem_limit_bytes=40 * 1024 * 1024),
        name="pair_step",
    )(left, right, got, pair_grad, *mats)


def on_device(pooled, field_owner, w_squeeze, w_excite, w_bilinear, tower_weight, tower_cotangent):
    f32, bf16 = jnp.float32, jnp.bfloat16
    per_owner, _, _, width, samples = pooled.shape
    tables, subs = lax.axis_size("table"), lax.axis_size("sub")
    total_samples = tables * subs * samples
    count = field_owner.shape[0]
    rows, hidden = tower_weight.shape
    plan = make_plan(count, tables, subs, width, rows)
    plane, depth, unit, units = plan["plane"], plan["depth"], plan["unit"], plan["units"]
    quarter = hidden // subs
    scale = 1.0 / width**0.5
    signs_np = hadamard_np(width)
    signs = jnp.asarray(signs_np, bf16)
    here = lax.axis_index("table")

    rotated = (
        jnp.einsum("ij,ktsjb->ktsib", signs, pooled, preferred_element_type=f32) * scale
    ).astype(bf16)
    rotated, tower_weight = lax.optimization_barrier((rotated, tower_weight))
    received = lax.all_to_all(rotated, "table", split_axis=1, concat_axis=0, tiled=True)
    received = received.reshape(per_owner * tables, width, samples)

    cut = jnp.moveaxis(tower_weight.reshape(rows, subs, quarter), 1, 0)
    cut = xor_order(cut, "sub")
    cut = trade([cut[k] for k in range(subs)], "sub", subs)

    slot_index = slot_table(field_owner, per_owner)
    table = jnp.asarray(plan["table"].reshape(-1))
    selected = jnp.take(received, slot_index, axis=0, mode="clip")
    squeeze_rows = selected[:, 0, :]

    cut = xor_order(jnp.stack(cut), "sub").reshape(units, unit, quarter)
    cut = jnp.concatenate([cut, jnp.zeros((1, unit, quarter), bf16)], axis=0)
    cut = jnp.take(cut, jnp.asarray(plan["pick"])[here], axis=0, mode="clip")
    cut = cut.reshape(plane, depth * width, quarter)
    cut = trade([cut[k] for k in range(plane)], "table", tables)
    cut = jnp.concatenate(cut, axis=0)

    sent = pack_rows(received, squeeze_rows, slot_index, table)
    sent, cut = lax.optimization_barrier((sent, cut))
    got = lax.all_to_all(sent, "table", split_axis=0, concat_axis=0, tiled=True)
    pieces = trade([cut] * subs, "sub", subs)

    cotangent = lax.all_gather(tower_cotangent, "table", axis=1, tiled=True)
    own_sub = lax.axis_index("sub")
    pair_grad = tower_pairs(own_sub[None], pieces, cotangent)

    xh, xl = halves(w_excite)
    mine = jnp.asarray(plan["table"])[here]
    here_h, here_l = [
        jnp.take(x.reshape(count, width, -1), mine, axis=0, mode="clip").reshape(LIMIT * width, -1)
        for x in (xh, xl)
    ]
    s1, s2 = halves(w_squeeze)
    s3 = (w_squeeze - s1.astype(f32) - s2.astype(f32)).astype(bf16)
    w_sq = jnp.concatenate([s1, s2, s3], axis=1)
    pairs, part, d_bilinear, d_excite, d_squeeze = pair_step(
        got,
        pair_grad,
        jnp.asarray(plan["left"])[here],
        jnp.asarray(plan["right"])[here],
        signs_np,
        jnp.stack([*halves(w_bilinear.T), *halves(w_bilinear)]),
        jnp.concatenate([here_h, here_l, here_h], axis=1),
        jnp.concatenate([here_h, here_h, here_l], axis=0).T,
        w_sq,
        width,
    )
    parts = lax.all_to_all(part, "table", split_axis=0, concat_axis=0, tiled=True)

    total = lax.dot_general(
        pairs, cotangent, (((1,), (1,)), ((), ())), preferred_element_type=f32
    )
    total = jnp.moveaxis(total.astype(bf16).reshape(-1, subs, quarter), 1, 0)
    total = xor_order(total, "sub")
    total = trade([total[k] for k in range(subs)], "sub", subs)
    total = sum(x.astype(f32) for x in total) * (1.0 / total_samples)
    total = total.astype(bf16).reshape(plane, depth * width, quarter)
    total = trade([total[k] for k in range(plane)], "table", tables)
    total = jnp.concatenate(total, axis=0).reshape(-1, unit, quarter)
    total = jnp.take(total, jnp.asarray(plan["back"])[here], axis=0, mode="clip")
    total = xor_order(total.reshape(subs, rows, quarter), "sub")
    total = trade([total[k] for k in range(subs)], "sub", subs)
    total = xor_order(jnp.stack(total), "sub")
    weight_grad = jnp.moveaxis(total, 0, 1).reshape(rows, hidden).astype(f32)

    hidden_units = w_squeeze.shape[0]
    half = d_bilinear.shape[1]
    d_bilinear = sum(
        d_bilinear[k : k + width, k % half : k % half + width]
        for k in range(0, LIMIT * width, width)
    )
    d_excite = d_excite[:hidden_units] + d_excite[hidden_units:]
    d_squeeze = (d_squeeze[:hidden_units] + d_squeeze[hidden_units:]) * scale
    lift = (jnp.arange(count, dtype=jnp.int32)[:, None] == mine[None, :]) & jnp.asarray(
        plan["live"]
    )[here][None, :]
    d_excite = d_excite.reshape(hidden_units, LIMIT, width).transpose(1, 2, 0)
    d_excite = jnp.dot(
        lift.astype(f32), d_excite.reshape(LIMIT, width * hidden_units), precision=HIGH
    )
    small = jnp.concatenate([d_excite.reshape(-1), d_squeeze.reshape(-1), d_bilinear.reshape(-1)])
    ends = np.cumsum([w_excite.size, w_squeeze.size, w_bilinear.size])
    small = jnp.pad(small, (0, -small.size % 1024)).reshape(-1, 128)
    for axis, size in (("table", tables), ("sub", subs)):
        bit = 1
        while bit < size:
            small = small + swap(small, axis, size, bit)
            bit *= 2
    small = small.reshape(-1) * (1.0 / total_samples)
    g_excite = small[: ends[0]].reshape(w_excite.shape)
    g_squeeze = small[ends[0] : ends[1]].reshape(w_squeeze.shape)
    g_bilinear = small[ends[1] : ends[2]].reshape(w_bilinear.shape)

    bundled = [x.T.reshape(hidden_units, count // 8, 8 * width).transpose(1, 0, 2) for x in (xh, xl)]
    placed = owner_step(
        parts,
        selected,
        squeeze_rows,
        table,
        slot_index,
        jnp.concatenate([xh, xl, xh], axis=1),
        jnp.stack(bundled, axis=1),
        w_sq,
        jnp.concatenate([s1, s1, s2], axis=0).T,
        per_owner * tables,
    )
    placed = placed.reshape(per_owner * tables, 1, 1, width, samples)
    row_grads = lax.all_to_all(placed, "table", split_axis=0, concat_axis=1, tiled=True)
    return (row_grads, weight_grad, g_squeeze, g_excite, g_bilinear)


def solution(mesh):
    return jax.shard_map(
        on_device,
        mesh=mesh,
        in_specs=(
            P("table", None, "sub", None, None),
            P(),
            P(),
            P(),
            P(),
            P(BOTH, None),
            P(None, BOTH),
        ),
        out_specs=(P("table", None, "sub", None, None), P(BOTH, None), P(), P(), P()),
        check_vma=False,
    )
```

profile of v0, /device:TPU:10, one launch (start us, length us, event | category | flops | bytes accessed | tf_op | source)
XLA Modules:
  0.0 321.5 jit_solution(1746199219059481839)
XLA Ops:
  8.3 1.0 fusion.4
  9.3 1.7 reshape.148
  12.4 2.6 collective-permute-start.1
  16.4 8.5 %all-to-all-start = ((bf16[3,32,1,32,128]{4,3,0,2,1:T(8,128)(2,1)}), bf16[3,32,1,32,128]{4,3,0,2,1:T(8,128)(2,1)S(1)}, u32[]{:S(2)}, u32[]{:S(2)}) async-start(bf16[3,32,1,32,128]{4,3,0,2,1:T(8,128)(2,1)} %copy.156), calls=%async_computation | async-start | bytes 1572864 | tf_op jit(solution)/shard_map/all_to_all | solution.py:436
  28.8 1.4 collective-permute-start.5
  30.1 2.1 collective-permute-start.6
  32.2 1.2 collective-permute-start.7
  33.4 1.5 collective-permute-start.8
  34.9 4.7 %collective-permute-done.4 = bf16[160,256]{1,0:T(8,128)(2,1)S(1)} collective-permute-done((bf16[160,256]{1,0:T(8,128)(2,1)S(1)}, bf16[160,256]{1,0:T(8,128)(2,1)S(1)}, u32[]{:S(2)}, u32[]{:S(2)}) %collective-permute-start.4) | collective-permute-done | bytes 81952 | tf_op jit(solution)/shard_map/ppermute | solution.py:115
  39.6 1.1 collective-permute-start.9
  40.8 4.4 %collective-permute-done.6 = bf16[160,256]{1,0:T(8,128)(2,1)S(1)} collective-permute-done((bf16[160,256]{1,0:T(8,128)(2,1)S(1)}, bf16[160,256]{1,0:T(8,128)(2,1)S(1)}, u32[]{:S(2)}, u32[]{:S(2)}) %collective-permute-start.6) | collective-permute-done | bytes 81952 | tf_op jit(solution)/shard_map/ppermute | solution.py:115
  45.8 1.4 collective-permute-done.9
  48.5 4.4 %pack_rows.1 = bf16[32,464,128]{2,1,0:T(8,128)(2,1)} custom-call(s32[48]{0:T(128)} %copy-done.14, s32[416]{0:T(512)} %constant.52.clone.table_ref, bf16[96,32,128]{2,1,0:T(8,128)(2,1)} %bitcast.167, bf16[48,128]{1,0:T(8,128)(2,1)} %bitcast.163), custom_call_target="tpu_custom_call" | custom-call | tf_op jit(solution)/shard_map/pack_rows/pallas_call | solution.py:148
  52.9 7.5 %all-to-all-start.1 = ((bf16[32,464,128]{2,1,0:T(8,128)(2,1)}), bf16[32,464,128]{2,1,0:T(8,128)(2,1)}, u32[]{:S(2)}, u32[]{:S(2)}) async-start(bf16[32,464,128]{2,1,0:T(8,128)(2,1)} %pack_rows.1), calls=%async_computation.1 | async-start | bytes 7602176 | tf_op jit(solution)/shard_map/all_to_all | solution.py:457
  63.8 1.8 collective-permute-start.10
  65.6 1.9 collective-permute-start.11
  69.4 12.1 %collective-permute-done.10.refs_1_ = bf16[1280,256]{1,0:T(8,128)(2,1)S(1)} collective-permute-done((bf16[1280,256]{1,0:T(8,128)(2,1)S(1)}, bf16[1280,256]{1,0:T(8,128)(2,1)S(1)}, u32[]{:S(2)}, u32[]{:S(2)}) %collective-permute-start.10) | collective-permute-done | bytes 655392 | tf_op jit(solution)/shard_map/ppermute | solution.py:115
  81.5 15.1 %collective-permute-done.11.refs_2_ = bf16[1280,256]{1,0:T(8,128)(2,1)S(1)} collective-permute-done((bf16[1280,256]{1,0:T(8,128)(2,1)S(1)}, bf16[1280,256]{1,0:T(8,128)(2,1)S(1)}, u32[]{:S(2)}, u32[]{:S(2)}) %collective-permute-start.11) | collective-permute-done | bytes 655392 | tf_op jit(solution)/shard_map/ppermute | solution.py:115
  96.6 1.5 collective-permute-done.12.refs_3_
  98.9 14.4 %all-gather.2.cloned.1.call-done.refs_4_ = bf16[1024,4096]{1,0:T(8,128)(2,1)} async-done(((bf16[1024,128]{1,0:T(8,128)(2,1)}), bf16[1024,4096]{1,0:T(8,128)(2,1)}) %all-gather.2.cloned.1.call-update) | async-done | bytes 8388624 | tf_op jit(solution)/shard_map/all_gather | solution.py:460
  113.3 3.4 %copy-done.16 = bf16[1024,4096]{1,0:T(8,128)(2,1)S(1)} copy-done((bf16[1024,4096]{1,0:T(8,128)(2,1)S(1)}, bf16[1024,4096]{1,0:T(8,128)(2,1)}, u32[]{:S(2)}) %copy-start.16) | copy-done | bytes 8388632
  116.7 1.1 copy-done.18
  117.8 14.4 %tower_pairs.1.pg_ref = bf16[1280,4096]{1,0:T(8,128)(2,1)} custom-call(s32[1]{0:T(128)} %bitcast.31.own_ref, bf16[1280,256]{1,0:T(8,128)(2,1)S(1)} %constant_dynamic-update-slice_fusion.refs_0_, bf16[1280,256]{1,0:T(8,128)(2,1)S(1)} %collective-permute-done.10.refs_1_, bf16[1280,256]{1,0:T(8,128)(2,1)S(1)} %collective-permute-done.11.refs_2_, ...), custom_call_target="tpu_custom_call" | custom-call | flops 10737418240 | bytes 30000000 | tf_op jit(solution)/shard_map/tower_pairs/pallas_call | solution.py:186
  132.3 26.1 %pair_step.1 = (bf16[1280,4096]{1,0:T(8,128)(2,1)}, bf16[32,416,128]{2,1,0:T(8,128)(2,1)S(1)}, f32[416,224]{1,0:T(8,128)S(1)}, f32[32,416]{1,0:T(8,128)S(1)}, f32[32,48]{1,0:T(8,128)S(1)}) custom-call(s32[40]{0:T(128)S(1)} %get-tuple-element.85.left_ref, s32[40]{0:T(128)S(1)} %get-tuple-element.86.right_ref, bf16[32,464,128]{2,1,0:T(8,128)(2,1)} %all-to-all-done.1.got_ref, ...), custom_call_target="tpu_custom_call" | custom-call | tf_op jit(solution)/shard_map/pair_step/pallas_call | solution.py:383
  158.4 1.8 copy-done.2
  162.0 17.4 %convolution_convert_fusion = bf16[1280,1024]{0,1:T(8,128)(2,1)} fusion(bf16[1280,4096]{1,0:T(8,128)(2,1)} %get-tuple-element.19, bf16[1024,4096]{1,0:T(8,128)(2,1)} %all-gather.2.cloned.1.call-done.refs_4_), kind=kOutput, calls=%fused_computation.10 | convolution fusion | flops 10738728960 | bytes 21495808 | tf_op jit(solution)/shard_map/dot_general | solution.py:487
  179.4 3.0 copy.176
  182.3 2.2 gather_fusion.6
  184.5 9.1 %all-to-all-start.2 = ((bf16[32,416,128]{2,1,0:T(8,128)(2,1)}), bf16[32,416,128]{2,1,0:T(8,128)(2,1)S(1)}, u32[]{:S(2)}, u32[]{:S(2)}) async-start(bf16[32,416,128]{2,1,0:T(8,128)(2,1)} %copy-done.2), calls=%async_computation.2 | async-start | bytes 6815744 | tf_op jit(solution)/shard_map/all_to_all | solution.py:485
  193.6 2.8 slice_bitcast_fusion.2
  197.0 2.4 collective-permute-start.14
  200.0 1.6 fusion.21
  202.4 1.9 copy.173.wex_ref
  204.3 30.5 %collective-permute-done.27 = f32[208,128]{1,0:T(8,128)} collective-permute-done((f32[208,128]{1,0:T(8,128)}, f32[208,128]{1,0:T(8,128)}, u32[]{:S(2)}, u32[]{:S(2)}) %collective-permute-start.27) | collective-permute-done | bytes 106528 | tf_op jit(solution)/shard_map/ppermute | solution.py:115
  234.7 1.0 fusion.29
  235.7 4.5 %collective-permute-start.28 = (f32[208,128]{1,0:T(8,128)S(1)}, f32[208,128]{1,0:T(8,128)S(1)}, u32[]{:S(2)}, u32[]{:S(2)}) collective-permute-start(f32[208,128]{1,0:T(8,128)S(1)} %fusion.29), channel_id=1, source_target_pairs={{0,16},{4,20},{8,24},{12,28},{16,0},{20,4},{24,8},{28,12},{32,48},... | collective-permute-start | bytes 319496 | tf_op jit(solution)/shard_map/ppermute | solution.py:115
  241.1 1.8 collective-permute-done.28
  242.9 1.9 collective-permute-start.29
  244.9 2.8 collective-permute-done.29
  247.7 3.1 collective-permute-start.30
  251.5 2.5 collective-permute-done.30
  254.9 2.0 fusion.3
  257.6 1.4 collective-permute-done.31
  259.7 2.1 collective-permute-start.32
  262.4 3.4 %collective-permute-start.19 = (bf16[160,256]{1,0:T(8,128)(2,1)S(1)}, bf16[160,256]{1,0:T(8,128)(2,1)S(1)}, u32[]{:S(2)}, u32[]{:S(2)}) collective-permute-start(bf16[160,256]{1,0:T(8,128)(2,1)S(1)} %get-tuple-element.61), channel_id=1, source_target_pairs={{0,16},{4,20},{8,24},{12,28},{16,0},{20,4},{24,8},{28,12},{32,48},... | collective-permute-start | bytes 245768 | tf_op jit(solution)/shard_map/ppermute | solution.py:115
  265.8 1.3 collective-permute-start.20
  267.7 1.8 collective-permute-start.21
  273.1 1.6 collective-permute-done.21
  275.4 1.1 collective-permute-done.22
  277.2 2.6 gather_fusion.7
  279.8 2.0 reshape.159
  281.8 2.5 gather_fusion.8
  284.3 1.0 copy-done.5
  285.3 1.0 copy-done.6
  287.2 4.0 %owner_step.1 = bf16[96,32,128]{2,1,0:T(8,128)(2,1)S(1)} custom-call(s32[416]{0:T(512)S(1)} %copy-done.13, s32[48]{0:T(128)S(1)} %copy-done.15, bf16[32,416,128]{2,1,0:T(8,128)(2,1)S(1)} %all-to-all-done.2.parts_ref, bf16[48,32,128]{2,1,0:T(8,128)(2,1)S(1)} %copy-done.5, bf16[48,128]{1,0:T(8,128)(2,1)S(1)} %bitcast.164, bf16[256,256]{1,0:T(8,128)(2,1)S(1)} %copy-done.9, ...), custom_call_target="tpu_custom_call" | custom-call | tf_op jit(solution)/shard_map/owner_step/pallas_call | solution.py:258
  292.1 7.0 %all-to-all-start.3 = ((bf16[96,1,1,32,128]{4,3,2,1,0:T(8,128)(2,1)}), bf16[96,1,1,32,128]{4,3,2,1,0:T(8,128)(2,1)S(1)}, u32[]{:S(2)}, u32[]{:S(2)}) async-start(bf16[96,1,1,32,128]{4,3,2,1,0:T(8,128)(2,1)} %bitcast.161), calls=%async_computation.3 | async-start | bytes 1572864 | tf_op jit(solution)/shard_map/all_to_all | solution.py:545
  299.2 1.2 fusion.23
  300.3 1.5 collective-permute-start.23
  301.9 2.0 collective-permute-start.25
  303.9 1.0 add_multiply_fusion
  307.4 1.8 collective-permute-done.24
  309.2 1.5 collective-permute-done.25
  312.4 1.2 copy.184
  313.7 0.9 copy.191
  (188 shorter events, 35.5 us)
Async XLA Ops:
  7.2 1.1 copy-start
  7.2 106.2 %all-gather.2.cloned.1.call-start = ((), (), s32[]{:S(2)}) async-start(), calls=%async_computation.4 | async-start | bytes 8650752 | tf_op jit(solution)/shard_map/all_gather | solution.py:460
  11.2 14.3 %copy-start.27 = (s32[48]{0:T(128)S(1)}, s32[48]{0:T(128)}, u32[]{:S(2)}) copy-start(s32[48]{0:T(128)} %param.21) | copy-start | bytes 580
  11.9 14.6 %collective-permute-start = (bf16[282,256]{1,0:T(8,128)(2,1)S(1)}, bf16[282,256]{1,0:T(8,128)(2,1)S(1)}, u32[]{:S(2)}, u32[]{:S(2)}) collective-permute-start(bf16[282,256]{1,0:T(8,128)(2,1)S(1)} %get-tuple-element.79), channel_id=1, source_target_pairs={{0,1},{1,0},{2,3},{3,2},{4,5},{5,4},{6,7},{7,6},{8,9},{9,8},{10,11... | collective-permute-start | bytes 433160 | tf_op jit(solution)/shard_map/ppermute | solution.py:115
  12.4 14.1 %collective-permute-start.1 = (bf16[282,256]{1,0:T(8,128)(2,1)S(1)}, bf16[282,256]{1,0:T(8,128)(2,1)S(1)}, u32[]{:S(2)}, u32[]{:S(2)}) collective-permute-start(bf16[282,256]{1,0:T(8,128)(2,1)S(1)} %get-tuple-element.78), channel_id=1, source_target_pairs={{0,2},{1,3},{2,0},{3,1},{4,6},{5,7},{6,4},{7,5},{8,10},{9,11},{10,... | collective-permute-start | bytes 433160 | tf_op jit(solution)/shard_map/ppermute | solution.py:115
  15.0 11.5 %collective-permute-start.2 = (bf16[282,256]{1,0:T(8,128)(2,1)S(1)}, bf16[282,256]{1,0:T(8,128)(2,1)S(1)}, u32[]{:S(2)}, u32[]{:S(2)}) collective-permute-start(bf16[282,256]{1,0:T(8,128)(2,1)S(1)} %get-tuple-element.80), channel_id=1, source_target_pairs={{0,3},{1,2},{2,1},{3,0},{4,7},{5,6},{6,5},{7,4},{8,11},{9,10},{10,... | collective-permute-start | bytes 433160 | tf_op jit(solution)/shard_map/ppermute | solution.py:115
  16.4 30.8 %all-to-all-start = ((bf16[3,32,1,32,128]{4,3,0,2,1:T(8,128)(2,1)}), bf16[3,32,1,32,128]{4,3,0,2,1:T(8,128)(2,1)S(1)}, u32[]{:S(2)}, u32[]{:S(2)}) async-start(bf16[3,32,1,32,128]{4,3,0,2,1:T(8,128)(2,1)} %copy.156), calls=%async_computation | async-start | bytes 1572864 | tf_op jit(solution)/shard_map/all_to_all | solution.py:436
  25.7 2.4 copy-start.14
  28.2 5.2 %collective-permute-start.3 = (bf16[160,256]{1,0:T(8,128)(2,1)S(1)}, bf16[160,256]{1,0:T(8,128)(2,1)S(1)}, u32[]{:S(2)}, u32[]{:S(2)}) collective-permute-start(bf16[160,256]{1,0:T(8,128)(2,1)S(1)} %get-tuple-element.72), channel_id=1, source_target_pairs={{0,4},{4,0},{8,12},{12,8},{16,20},{20,16},{24,28},{28,24},{32,36},... | collective-permute-start | bytes 245768 | tf_op jit(solution)/shard_map/ppermute | solution.py:115
  28.4 11.2 %collective-permute-start.4 = (bf16[160,256]{1,0:T(8,128)(2,1)S(1)}, bf16[160,256]{1,0:T(8,128)(2,1)S(1)}, u32[]{:S(2)}, u32[]{:S(2)}) collective-permute-start(bf16[160,256]{1,0:T(8,128)(2,1)S(1)} %get-tuple-element.71), channel_id=1, source_target_pairs={{0,8},{4,12},{8,0},{12,4},{16,24},{20,28},{24,16},{28,20},{32,40},... | collective-permute-start | bytes 245768 | tf_op jit(solution)/shard_map/ppermute | solution.py:115
  28.8 12.0 %collective-permute-start.5 = (bf16[160,256]{1,0:T(8,128)(2,1)S(1)}, bf16[160,256]{1,0:T(8,128)(2,1)S(1)}, u32[]{:S(2)}, u32[]{:S(2)}) collective-permute-start(bf16[160,256]{1,0:T(8,128)(2,1)S(1)} %get-tuple-element.70), channel_id=1, source_target_pairs={{0,12},{4,8},{8,4},{12,0},{16,28},{20,24},{24,20},{28,16},{32,44},... | collective-permute-start | bytes 245768 | tf_op jit(solution)/shard_map/ppermute | solution.py:115
  30.1 15.0 %collective-permute-start.6 = (bf16[160,256]{1,0:T(8,128)(2,1)S(1)}, bf16[160,256]{1,0:T(8,128)(2,1)S(1)}, u32[]{:S(2)}, u32[]{:S(2)}) collective-permute-start(bf16[160,256]{1,0:T(8,128)(2,1)S(1)} %get-tuple-element.69), channel_id=1, source_target_pairs={{0,16},{4,20},{8,24},{12,28},{16,0},{20,4},{24,8},{28,12},{32,48},... | collective-permute-start | bytes 245768 | tf_op jit(solution)/shard_map/ppermute | solution.py:115
  32.2 13.5 %collective-permute-start.7 = (bf16[160,256]{1,0:T(8,128)(2,1)S(1)}, bf16[160,256]{1,0:T(8,128)(2,1)S(1)}, u32[]{:S(2)}, u32[]{:S(2)}) collective-permute-start(bf16[160,256]{1,0:T(8,128)(2,1)S(1)} %get-tuple-element.68), channel_id=1, source_target_pairs={{0,20},{4,16},{8,28},{12,24},{16,4},{20,0},{24,12},{28,8},{32,52},... | collective-permute-start | bytes 245768 | tf_op jit(solution)/shard_map/ppermute | solution.py:115
  33.4 12.3 %collective-permute-start.8 = (bf16[160,256]{1,0:T(8,128)(2,1)S(1)}, bf16[160,256]{1,0:T(8,128)(2,1)S(1)}, u32[]{:S(2)}, u32[]{:S(2)}) collective-permute-start(bf16[160,256]{1,0:T(8,128)(2,1)S(1)} %get-tuple-element.67), channel_id=1, source_target_pairs={{0,24},{4,28},{8,16},{12,20},{16,8},{20,12},{24,0},{28,4},{32,56},... | collective-permute-start | bytes 245768 | tf_op jit(solution)/shard_map/ppermute | solution.py:115
  39.6 7.6 %collective-permute-start.9 = (bf16[160,256]{1,0:T(8,128)(2,1)S(1)}, bf16[160,256]{1,0:T(8,128)(2,1)S(1)}, u32[]{:S(2)}, u32[]{:S(2)}) collective-permute-start(bf16[160,256]{1,0:T(8,128)(2,1)S(1)} %get-tuple-element.66), channel_id=1, source_target_pairs={{0,28},{4,24},{8,20},{12,16},{16,12},{20,8},{24,4},{28,0},{32,60},... | collective-permute-start | bytes 245768 | tf_op jit(solution)/shard_map/ppermute | solution.py:115
  47.2 1.4 copy-start.19
  47.8 5.1 %copy-start.4 = (bf16[48,32,128]{2,1,0:T(8,128)(2,1)}, bf16[48,32,128]{2,1,0:T(8,128)(2,1)S(1)}, u32[]{:S(2)}) copy-start(bf16[48,32,128]{2,1,0:T(8,128)(2,1)S(1)} %gather_fusion) | copy-start | bytes 1179652
  52.9 7.5 %copy-start.26 = (f32[16,48]{1,0:T(8,128)S(1)}, f32[16,48]{1,0:T(8,128)}, u32[]{:S(2)}) copy-start(f32[16,48]{1,0:T(8,128)} %param.22) | copy-start | bytes 9220
  52.9 7.6 %copy-start.24 = (f32[1536,16]{0,1:T(8,128)S(1)}, f32[1536,16]{0,1:T(8,128)}, u32[]{:S(2)}) copy-start(f32[1536,16]{0,1:T(8,128)} %param.23) | copy-start | bytes 294916
  52.9 79.4 %all-to-all-start.1 = ((bf16[32,464,128]{2,1,0:T(8,128)(2,1)}), bf16[32,464,128]{2,1,0:T(8,128)(2,1)}, u32[]{:S(2)}, u32[]{:S(2)}) async-start(bf16[32,464,128]{2,1,0:T(8,128)(2,1)} %pack_rows.1), calls=%async_computation.1 | async-start | bytes 7602176 | tf_op jit(solution)/shard_map/all_to_all | solution.py:457
  60.4 2.5 copy-start.25
  60.6 71.7 %copy-start.20 = (bf16[1536,16]{0,1:T(8,128)(2,1)}, bf16[1536,16]{0,1:T(8,128)(2,1)S(1)}, u32[]{:S(2)}) copy-start(bf16[1536,16]{0,1:T(8,128)(2,1)S(1)} %get-tuple-element.53) | copy-start | bytes 147460
  60.6 71.7 %copy-start.22 = (bf16[1536,16]{0,1:T(8,128)(2,1)}, bf16[1536,16]{0,1:T(8,128)(2,1)S(1)}, u32[]{:S(2)}) copy-start(bf16[1536,16]{0,1:T(8,128)(2,1)S(1)} %get-tuple-element.54) | copy-start | bytes 147460
  63.8 17.7 %collective-permute-start.10 = (bf16[1280,256]{1,0:T(8,128)(2,1)S(1)}, bf16[1280,256]{1,0:T(8,128)(2,1)S(1)}, u32[]{:S(2)}, u32[]{:S(2)}) collective-permute-start(bf16[1280,256]{1,0:T(8,128)(2,1)S(1)} %constant_dynamic-update-slice_fusion.refs_0_), channel_id=1, source_target_pairs={{0,1},{1,0},{2,3},{3,2},{4,5},{5,4},{6,7},{7,6},{8,9},{9,8},{10,11... | collective-permute-start | bytes 1966088 | tf_op jit(solution)/shard_map/ppermute | solution.py:115
  65.6 31.0 %collective-permute-start.11 = (bf16[1280,256]{1,0:T(8,128)(2,1)S(1)}, bf16[1280,256]{1,0:T(8,128)(2,1)S(1)}, u32[]{:S(2)}, u32[]{:S(2)}) collective-permute-start(bf16[1280,256]{1,0:T(8,128)(2,1)S(1)} %constant_dynamic-update-slice_fusion.refs_0_), channel_id=1, source_target_pairs={{0,2},{1,3},{2,0},{3,1},{4,6},{5,7},{6,4},{7,5},{8,10},{9,11},{10,... | collective-permute-start | bytes 1966088 | tf_op jit(solution)/shard_map/ppermute | solution.py:115
  67.6 30.5 %collective-permute-start.12 = (bf16[1280,256]{1,0:T(8,128)(2,1)S(1)}, bf16[1280,256]{1,0:T(8,128)(2,1)S(1)}, u32[]{:S(2)}, u32[]{:S(2)}) collective-permute-start(bf16[1280,256]{1,0:T(8,128)(2,1)S(1)} %constant_dynamic-update-slice_fusion.refs_0_), channel_id=1, source_target_pairs={{0,3},{1,2},{2,1},{3,0},{4,7},{5,6},{6,5},{7,4},{8,11},{9,10},{10,... | collective-permute-start | bytes 1966088 | tf_op jit(solution)/shard_map/ppermute | solution.py:115
  113.3 3.4 %copy-start.16 = (bf16[1024,4096]{1,0:T(8,128)(2,1)S(1)}, bf16[1024,4096]{1,0:T(8,128)(2,1)}, u32[]{:S(2)}) copy-start(bf16[1024,4096]{1,0:T(8,128)(2,1)} %all-gather.2.cloned.1.call-done.refs_4_) | copy-start | bytes 25165828
  116.7 1.1 copy-start.18
  117.8 14.5 %copy-start.7 = (f32[416,224]{1,0:T(8,128)S(1)}, f32[416,224]{1,0:T(8,128)}, u32[]{:S(2)}) copy-start(f32[416,224]{1,0:T(8,128)} %constant.60.clone.mask_ref) | copy-start | bytes 1118212
  117.8 14.5 %copy-start.8 = (bf16[416,224]{1,0:T(8,128)(2,1)S(1)}, bf16[416,224]{1,0:T(8,128)(2,1)}, u32[]{:S(2)}) copy-start(bf16[416,224]{1,0:T(8,128)(2,1)} %constant.57.clone.hd_ref) | copy-start | bytes 559108
  117.8 14.5 %copy-start.11 = (bf16[416,32]{1,0:T(8,128)(2,1)S(1)}, bf16[416,32]{1,0:T(8,128)(2,1)}, u32[]{:S(2)}) copy-start(bf16[416,32]{1,0:T(8,128)(2,1)} %constant.58.clone.rep_ref) | copy-start | bytes 79876
  117.8 14.5 %copy-start.12 = (bf16[32,224]{1,0:T(8,128)(2,1)S(1)}, bf16[32,224]{1,0:T(8,128)(2,1)}, u32[]{:S(2)}) copy-start(bf16[32,224]{1,0:T(8,128)(2,1)} %constant.59.clone.rept_ref) | copy-start | bytes 43012
  158.4 1.8 copy-start.2
  161.7 38.2 %collective-permute-start.26 = (f32[208,128]{1,0:T(8,128)}, f32[208,128]{1,0:T(8,128)}, u32[]{:S(2)}, u32[]{:S(2)}) collective-permute-start(f32[208,128]{1,0:T(8,128)} %fusion.6), channel_id=1, source_target_pairs={{0,4},{4,0},{8,12},{12,8},{16,20},{20,16},{24,28},{28,24},{32,36},... | collective-permute-start | bytes 319496 | tf_op jit(solution)/shard_map/ppermute | solution.py:115
  184.5 99.8 %all-to-all-start.2 = ((bf16[32,416,128]{2,1,0:T(8,128)(2,1)}), bf16[32,416,128]{2,1,0:T(8,128)(2,1)S(1)}, u32[]{:S(2)}, u32[]{:S(2)}) async-start(bf16[32,416,128]{2,1,0:T(8,128)(2,1)} %copy-done.2), calls=%async_computation.2 | async-start | bytes 6815744 | tf_op jit(solution)/shard_map/all_to_all | solution.py:485
  193.6 8.2 %copy-start.21 = (bf16[1536,16]{0,1:T(8,128)(2,1)S(1)}, bf16[1536,16]{0,1:T(8,128)(2,1)}, u32[]{:S(2)}) copy-start(bf16[1536,16]{0,1:T(8,128)(2,1)} %copy-done.20) | copy-start | bytes 147460
  193.6 8.1 %copy-start.23 = (bf16[1536,16]{0,1:T(8,128)(2,1)S(1)}, bf16[1536,16]{0,1:T(8,128)(2,1)}, u32[]{:S(2)}) copy-start(bf16[1536,16]{0,1:T(8,128)(2,1)} %copy-done.22) | copy-start | bytes 147460
  196.5 58.4 %collective-permute-start.13 = (bf16[1280,256]{1,0:T(8,128)(2,1)}, bf16[1280,256]{1,0:T(8,128)(2,1)}, u32[]{:S(2)}, u32[]{:S(2)}) collective-permute-start(bf16[1280,256]{1,0:T(8,128)(2,1)} %get-tuple-element.55), channel_id=1, source_target_pairs={{0,1},{1,0},{2,3},{3,2},{4,5},{5,4},{6,7},{7,6},{8,9},{9,8},{10,11... | collective-permute-start | bytes 1966088 | tf_op jit(solution)/shard_map/ppermute | solution.py:115
  197.0 57.9 %collective-permute-start.14 = (bf16[1280,256]{1,0:T(8,128)(2,1)}, bf16[1280,256]{1,0:T(8,128)(2,1)}, u32[]{:S(2)}, u32[]{:S(2)}) collective-permute-start(bf16[1280,256]{1,0:T(8,128)(2,1)} %get-tuple-element.56), channel_id=1, source_target_pairs={{0,2},{1,3},{2,0},{3,1},{4,6},{5,7},{6,4},{7,5},{8,10},{9,11},{10,... | collective-permute-start | bytes 1966088 | tf_op jit(solution)/shard_map/ppermute | solution.py:115
  199.4 55.5 %collective-permute-start.15 = (bf16[1280,256]{1,0:T(8,128)(2,1)}, bf16[1280,256]{1,0:T(8,128)(2,1)}, u32[]{:S(2)}, u32[]{:S(2)}) collective-permute-start(bf16[1280,256]{1,0:T(8,128)(2,1)} %get-tuple-element.57), channel_id=1, source_target_pairs={{0,3},{1,2},{2,1},{3,0},{4,7},{5,6},{6,5},{7,4},{8,11},{9,10},{10,... | collective-permute-start | bytes 1966088 | tf_op jit(solution)/shard_map/ppermute | solution.py:115
  201.5 33.2 %collective-permute-start.27 = (f32[208,128]{1,0:T(8,128)}, f32[208,128]{1,0:T(8,128)}, u32[]{:S(2)}, u32[]{:S(2)}) collective-permute-start(f32[208,128]{1,0:T(8,128)} %fusion.21), channel_id=1, source_target_pairs={{0,8},{4,12},{8,0},{12,4},{16,24},{20,28},{24,16},{28,20},{32,40},... | collective-permute-start | bytes 319496 | tf_op jit(solution)/shard_map/ppermute | solution.py:115
  235.7 7.2 %collective-permute-start.28 = (f32[208,128]{1,0:T(8,128)S(1)}, f32[208,128]{1,0:T(8,128)S(1)}, u32[]{:S(2)}, u32[]{:S(2)}) collective-permute-start(f32[208,128]{1,0:T(8,128)S(1)} %fusion.29), channel_id=1, source_target_pairs={{0,16},{4,20},{8,24},{12,28},{16,0},{20,4},{24,8},{28,12},{32,48},... | collective-permute-start | bytes 319496 | tf_op jit(solution)/shard_map/ppermute | solution.py:115
  242.9 4.8 %collective-permute-start.29 = (f32[208,128]{1,0:T(8,128)S(1)}, f32[208,128]{1,0:T(8,128)S(1)}, u32[]{:S(2)}, u32[]{:S(2)}) collective-permute-start(f32[208,128]{1,0:T(8,128)S(1)} %add.108), channel_id=1, source_target_pairs={{0,32},{4,36},{8,40},{12,44},{16,48},{20,52},{24,56},{28,60},{32,0... | collective-permute-start | bytes 319496 | tf_op jit(solution)/shard_map/ppermute | solution.py:115
  247.7 6.3 %collective-permute-start.30 = (f32[208,128]{1,0:T(8,128)S(1)}, f32[208,128]{1,0:T(8,128)S(1)}, u32[]{:S(2)}, u32[]{:S(2)}) collective-permute-start(f32[208,128]{1,0:T(8,128)S(1)} %add.109), channel_id=1, source_target_pairs={{0,64},{4,68},{8,72},{12,76},{16,80},{20,84},{24,88},{28,92},{32,9... | collective-permute-start | bytes 319496 | tf_op jit(solution)/shard_map/ppermute | solution.py:115
  254.0 5.0 %collective-permute-start.31 = (f32[208,128]{1,0:T(8,128)S(1)}, f32[208,128]{1,0:T(8,128)S(1)}, u32[]{:S(2)}, u32[]{:S(2)}) collective-permute-start(f32[208,128]{1,0:T(8,128)S(1)} %add.110), channel_id=1, source_target_pairs={{0,1},{1,0},{2,3},{3,2},{4,5},{5,4},{6,7},{7,6},{8,9},{9,8},{10,11... | collective-permute-start | bytes 319496 | tf_op jit(solution)/shard_map/ppermute | solution.py:115
  257.6 26.7 %copy-start.10 = (bf16[48,1,128]{2,0,1:T(8,128)(2,1)S(1)}, bf16[48,1,128]{2,0,1:T(8,128)(2,1)}, u32[]{:S(2)}) copy-start(bf16[48,1,128]{2,0,1:T(8,128)(2,1)} %copy.193) | copy-start | bytes 36868
  257.6 26.7 %copy-start.13 = (s32[416]{0:T(512)S(1)}, s32[416]{0:T(512)}, u32[]{:S(2)}) copy-start(s32[416]{0:T(512)} %constant.52.clone.table_ref) | copy-start | bytes 4996
  257.6 26.7 %copy-start.15 = (s32[48]{0:T(128)S(1)}, s32[48]{0:T(128)}, u32[]{:S(2)}) copy-start(s32[48]{0:T(128)} %copy-done.14) | copy-start | bytes 580
  257.6 8.2 %collective-permute-start.16 = (bf16[160,256]{1,0:T(8,128)(2,1)S(1)}, bf16[160,256]{1,0:T(8,128)(2,1)S(1)}, u32[]{:S(2)}, u32[]{:S(2)}) collective-permute-start(bf16[160,256]{1,0:T(8,128)(2,1)S(1)} %get-tuple-element.64), channel_id=1, source_target_pairs={{0,4},{4,0},{8,12},{12,8},{16,20},{20,16},{24,28},{28,24},{32,36},... | collective-permute-start | bytes 245768 | tf_op jit(solution)/shard_map/ppermute | solution.py:115
  259.7 44.2 %collective-permute-start.32 = (f32[208,128]{1,0:T(8,128)}, f32[208,128]{1,0:T(8,128)}, u32[]{:S(2)}, u32[]{:S(2)}) collective-permute-start(f32[208,128]{1,0:T(8,128)} %add.111), channel_id=1, source_target_pairs={{0,2},{1,3},{2,0},{3,1},{4,6},{5,7},{6,4},{7,5},{8,10},{9,11},{10,... | collective-permute-start | bytes 319496 | tf_op jit(solution)/shard_map/ppermute | solution.py:115
  261.8 5.9 %collective-permute-start.17 = (bf16[160,256]{1,0:T(8,128)(2,1)S(1)}, bf16[160,256]{1,0:T(8,128)(2,1)S(1)}, u32[]{:S(2)}, u32[]{:S(2)}) collective-permute-start(bf16[160,256]{1,0:T(8,128)(2,1)S(1)} %get-tuple-element.63), channel_id=1, source_target_pairs={{0,8},{4,12},{8,0},{12,4},{16,24},{20,28},{24,16},{28,20},{32,40},... | collective-permute-start | bytes 245768 | tf_op jit(solution)/shard_map/ppermute | solution.py:115
  262.4 7.8 %collective-permute-start.18 = (bf16[160,256]{1,0:T(8,128)(2,1)S(1)}, bf16[160,256]{1,0:T(8,128)(2,1)S(1)}, u32[]{:S(2)}, u32[]{:S(2)}) collective-permute-start(bf16[160,256]{1,0:T(8,128)(2,1)S(1)} %get-tuple-element.62), channel_id=1, source_target_pairs={{0,12},{4,8},{8,4},{12,0},{16,28},{20,24},{24,20},{28,16},{32,44},... | collective-permute-start | bytes 245768 | tf_op jit(solution)/shard_map/ppermute | solution.py:115
  262.4 8.7 %collective-permute-start.19 = (bf16[160,256]{1,0:T(8,128)(2,1)S(1)}, bf16[160,256]{1,0:T(8,128)(2,1)S(1)}, u32[]{:S(2)}, u32[]{:S(2)}) collective-permute-start(bf16[160,256]{1,0:T(8,128)(2,1)S(1)} %get-tuple-element.61), channel_id=1, source_target_pairs={{0,16},{4,20},{8,24},{12,28},{16,0},{20,4},{24,8},{28,12},{32,48},... | collective-permute-start | bytes 245768 | tf_op jit(solution)/shard_map/ppermute | solution.py:115
  265.8 6.7 %collective-permute-start.20 = (bf16[160,256]{1,0:T(8,128)(2,1)S(1)}, bf16[160,256]{1,0:T(8,128)(2,1)S(1)}, u32[]{:S(2)}, u32[]{:S(2)}) collective-permute-start(bf16[160,256]{1,0:T(8,128)(2,1)S(1)} %get-tuple-element.60), channel_id=1, source_target_pairs={{0,20},{4,16},{8,28},{12,24},{16,4},{20,0},{24,12},{28,8},{32,52},... | collective-permute-start | bytes 245768 | tf_op jit(solution)/shard_map/ppermute | solution.py:115
  267.7 7.1 %collective-permute-start.21 = (bf16[160,256]{1,0:T(8,128)(2,1)S(1)}, bf16[160,256]{1,0:T(8,128)(2,1)S(1)}, u32[]{:S(2)}, u32[]{:S(2)}) collective-permute-start(bf16[160,256]{1,0:T(8,128)(2,1)S(1)} %get-tuple-element.59), channel_id=1, source_target_pairs={{0,24},{4,28},{8,16},{12,20},{16,8},{20,12},{24,0},{28,4},{32,56},... | collective-permute-start | bytes 245768 | tf_op jit(solution)/shard_map/ppermute | solution.py:115
  270.2 6.3 %collective-permute-start.22 = (bf16[160,256]{1,0:T(8,128)(2,1)S(1)}, bf16[160,256]{1,0:T(8,128)(2,1)S(1)}, u32[]{:S(2)}, u32[]{:S(2)}) collective-permute-start(bf16[160,256]{1,0:T(8,128)(2,1)S(1)} %get-tuple-element.58), channel_id=1, source_target_pairs={{0,28},{4,24},{8,20},{12,16},{16,12},{20,8},{24,4},{28,0},{32,60},... | collective-permute-start | bytes 245768 | tf_op jit(solution)/shard_map/ppermute | solution.py:115
  284.3 1.0 copy-start.5
  285.3 1.0 copy-start.6
  286.3 0.9 copy-start.9
  292.1 21.5 %all-to-all-start.3 = ((bf16[96,1,1,32,128]{4,3,2,1,0:T(8,128)(2,1)}), bf16[96,1,1,32,128]{4,3,2,1,0:T(8,128)(2,1)S(1)}, u32[]{:S(2)}, u32[]{:S(2)}) async-start(bf16[96,1,1,32,128]{4,3,2,1,0:T(8,128)(2,1)} %bitcast.161), calls=%async_computation.3 | async-start | bytes 1572864 | tf_op jit(solution)/shard_map/all_to_all | solution.py:545
  300.3 7.1 %collective-permute-start.23 = (bf16[282,256]{1,0:T(8,128)(2,1)S(1)}, bf16[282,256]{1,0:T(8,128)(2,1)S(1)}, u32[]{:S(2)}, u32[]{:S(2)}) collective-permute-start(bf16[282,256]{1,0:T(8,128)(2,1)S(1)} %get-tuple-element.75), channel_id=1, source_target_pairs={{0,1},{1,0},{2,3},{3,2},{4,5},{5,4},{6,7},{7,6},{8,9},{9,8},{10,11... | collective-permute-start | bytes 433160 | tf_op jit(solution)/shard_map/ppermute | solution.py:115
  301.8 7.4 %collective-permute-start.24 = (bf16[282,256]{1,0:T(8,128)(2,1)S(1)}, bf16[282,256]{1,0:T(8,128)(2,1)S(1)}, u32[]{:S(2)}, u32[]{:S(2)}) collective-permute-start(bf16[282,256]{1,0:T(8,128)(2,1)S(1)} %get-tuple-element.74), channel_id=1, source_target_pairs={{0,2},{1,3},{2,0},{3,1},{4,6},{5,7},{6,4},{7,5},{8,10},{9,11},{10,... | collective-permute-start | bytes 433160 | tf_op jit(solution)/shard_map/ppermute | solution.py:115
  301.9 8.7 %collective-permute-start.25 = (bf16[282,256]{1,0:T(8,128)(2,1)S(1)}, bf16[282,256]{1,0:T(8,128)(2,1)S(1)}, u32[]{:S(2)}, u32[]{:S(2)}) collective-permute-start(bf16[282,256]{1,0:T(8,128)(2,1)S(1)} %get-tuple-element.76), channel_id=1, source_target_pairs={{0,3},{1,2},{2,1},{3,0},{4,7},{5,6},{6,5},{7,4},{8,11},{9,10},{10,... | collective-permute-start | bytes 433160 | tf_op jit(solution)/shard_map/ppermute | solution.py:115
  311.4 3.2 copy-start.1
  (2 other events, 1.7 us)
Sparse Core Ops, SparseCore 0:
  10.2 103.1 all-gather.1
where the time goes:
time: 326 us; the launch traced here: 321 us
  waiting for transfers between devices  101 us (31%)
  starting transfers between devices  75 us (23%)
  local copies, waits for them, and re-layouts  54.3 us (17%)
  Pallas kernels  49 us (15%)
  matrix products  18.6 us (6%)
  between operations  14.7 us (5%)
  other arithmetic  9.22 us (3%)
    ppermute x33, waiting for transfers between devices, swap(): return lax.ppermute(value, axis, [(a, a ^ k) for a in range(size)])  85.5 us
    ppermute x33, starting transfers between devices, swap(): return lax.ppermute(value, axis, [(a, a ^ k) for a in range(size)])  42.9 us
    pallas_call x1, Pallas kernels, pair_step(): pl.pallas_call(body, out_shape=(jax.ShapeDtypeStruct((slots * width, tabl...  26.1 us
    unnamed x76, local copies, waits for them, and re-layouts  18.4 us
    dot_general x1, matrix products, on_device(): lax.dot_general(pairs, cotangent, (((1,), (1,)), ((), ())), preferred_ele...  17.4 us
    pallas_call x1, Pallas kernels, tower_pairs(): pl.pallas_call(body, out_shape=jax.ShapeDtypeStruct((tall, cols), cotange...  14.4 us
    all_gather x1, waiting for transfers between devices, on_device(): cotangent = lax.all_gather(tower_cotangent, 'table', axis=1, tiled=True)  14.4 us
    all_to_all x1, starting transfers between devices, on_device(): lax.all_to_all(part, 'table', split_axis=0, concat_axis=0, tiled=True)  9.08 us
  transfers between devices with their start and end apart: 38, of which 18 were waited for; matrix products, arithmetic and copies ran while one was open for 21% of the time, Pallas kernels for 7%

commit v1 on v0

--- a/solution.py
+++ b/solution.py
@@ -27,12 +27,12 @@
     3, 5, 3, 7, 5, 3, 2, 4, 1, 5, 3, 2, 2, 1, 5, 7, 0, 6, 4, 2, 1, 5, 2, 1, 4, 7, 0, 6, 0, 6, 3, 4, 7, 1, 7, 6, 0, 3, 5, 5, 4, 3, 2, 4, 1, 5, 3,
     2, 2, 1, 5, 7, 0, 6, 4, 0, 1, 5, 2, 1, 4, 7, 0, 6, 0, 6, 3, 4, 7, 1, 7, 3, 0, 3, 5, 2, 3, 2, 4, 1, 5, 3, 2, 2, 1, 5, 7, 0, 6, 4, 0, 1, 5, 2,
     1, 4, 7, 0, 6, 0, 6, 3, 4, 7, 1, 7, 6, 0, 3, 5, 3, 2, 4, 1, 5, 3, 2, 2, 1, 5, 7, 0, 6, 4, 2, 1, 5, 2, 1, 4, 7, 0, 6, 0, 6, 3, 4, 7, 1, 7, 6,
-    0, 0, 0, 4, 2, 7, 7, 3, 5, 6, 4, 2, 5, 1, 3, 6, 1, 6, 7, 3, 4, 3, 1, 1, 4, 5, 7, 6, 1, 2, 4, 5, 7, 5, 2, 2, 4, 0, 0, 2, 0, 6, 1, 3, 5, 1, 3,
-    6, 1, 6, 7, 3, 4, 3, 1, 5, 4, 5, 7, 6, 2, 0, 4, 1, 7, 5, 0, 2, 4, 3, 7, 3, 1, 1, 6, 0, 1, 3, 6, 2, 6, 7, 3, 4, 3, 2, 1, 4, 0, 7, 6, 2, 0, 4,
-    1, 7, 0, 2, 2, 0, 7, 3, 4, 4, 6, 5, 5, 3, 6, 2, 6, 7, 3, 4, 3, 2, 5, 4, 0, 7, 6, 2, 0, 4, 5, 7, 5, 2, 0, 7, 0, 1, 4, 4, 0, 1, 3, 6, 1, 6, 7,
-    3, 4, 3, 1, 1, 4, 0, 7, 6, 1, 0, 4, 1, 7, 0, 0, 0, 6, 2, 7, 2, 5, 5, 3, 6, 2, 6, 7, 3, 4, 3, 2, 5, 4, 5, 7, 6, 2, 2, 4, 5, 7, 5, 2, 2, 3, 0,
-    6, 5, 1, 3, 6, 1, 6, 7, 3, 4, 3, 1, 1, 4, 0, 7, 6, 1, 0, 4, 5, 7, 0, 0, 0, 3, 4, 5, 1, 3, 6, 2, 6, 7, 3, 4, 3, 1, 5, 4, 5, 7, 6, 2, 2, 4, 5,
-    7, 5, 2, 2, 7, 0, 1, 3, 6, 1, 6, 7, 3, 4, 3, 1, 1, 4, 0, 7, 6, 1, 0, 4, 1, 7, 0, 0, 0, 5, 5, 3, 6, 2, 6, 7, 3, 4, 3, 2, 5, 4, 5, 7, 6, 2, 2,
+    7, 7, 7, 4, 1, 1, 5, 6, 0, 4, 4, 5, 6, 5, 6, 2, 6, 0, 2, 3, 0, 2, 1, 4, 0, 5, 2, 3, 3, 5, 3, 1, 1, 2, 6, 3, 1, 4, 7, 6, 1, 5, 5, 2, 0, 5, 6,
+    2, 6, 6, 0, 4, 2, 2, 1, 4, 0, 5, 2, 0, 0, 5, 4, 1, 1, 7, 7, 7, 4, 7, 6, 5, 4, 4, 3, 0, 5, 7, 4, 6, 6, 0, 3, 0, 7, 1, 3, 0, 5, 4, 3, 0, 5, 3,
+    1, 1, 7, 7, 7, 1, 5, 1, 6, 4, 2, 6, 5, 6, 4, 6, 6, 2, 3, 2, 2, 1, 4, 3, 5, 2, 3, 3, 5, 4, 1, 1, 2, 6, 3, 7, 4, 1, 1, 5, 0, 5, 7, 4, 7, 0, 0,
+    4, 0, 7, 1, 4, 0, 5, 4, 0, 0, 5, 4, 1, 1, 7, 7, 7, 6, 5, 7, 1, 6, 5, 6, 2, 6, 6, 2, 3, 2, 2, 1, 3, 3, 5, 2, 3, 3, 5, 3, 1, 1, 7, 6, 3, 2, 7,
+    5, 6, 5, 6, 4, 7, 0, 2, 4, 0, 2, 1, 4, 0, 5, 4, 0, 0, 5, 4, 1, 1, 7, 7, 7, 1, 2, 6, 5, 6, 4, 6, 6, 2, 4, 2, 2, 1, 4, 3, 5, 4, 3, 3, 5, 3, 1,
+    1, 2, 6, 3, 1, 0, 5, 7, 4, 7, 0, 0, 4, 0, 7, 1, 4, 0, 5, 4, 0, 0, 5, 4, 1, 1, 7, 7, 7, 6, 5, 6, 2, 6, 6, 2, 3, 2, 2, 1, 3, 3, 5, 2, 3, 3, 5,
     6, 6, 6, 1, 1, 1, 3, 5, 7, 5, 7, 0, 7, 0, 5, 0, 2, 3, 0, 5, 2, 0, 2, 5, 7, 3, 2, 7, 3, 3, 4, 2, 4, 1, 1, 4, 1, 3, 2, 3, 4, 2, 2, 4, 2, 4, 4,
     3, 2, 1, 1, 0, 6, 7, 5, 0, 0, 7, 3, 6, 6, 7, 5, 0, 5, 6, 7, 5, 6, 3, 7, 3, 6, 4, 6, 7, 3, 7, 0, 6, 7, 4, 3, 3, 0, 0, 4, 6, 4, 4, 7, 3, 1, 1,
     5, 2, 1, 2, 6, 1, 5, 2, 2, 1, 2, 5, 5, 6, 2, 6, 5, 1, 7, 4, 1, 4, 2, 7, 4, 2, 7, 1, 2, 4, 2, 7, 4, 7, 1, 5, 3, 0, 3, 6, 3, 0, 3, 0, 1, 6, 5,
@@ -204,6 +204,50 @@
     )(own, *pieces, cotangent)
 
 
+def tower_piece(own, pairs, cotangent, parts, k):
+    tall, cols = pairs.shape
+    quarter = cotangent.shape[0] // parts
+    step = 512
+
+    def body(own_ref, pairs_ref, cot_ref, out_ref, acc):
+        i = pl.program_id(0)
+
+        @pl.when(i == 0)
+        def _():
+            acc[...] = jnp.zeros_like(acc)
+
+        acc[...] += lax.dot_general(
+            pairs_ref[...],
+            cot_ref[...],
+            (((1,), (1,)), ((), ())),
+            preferred_element_type=jnp.float32,
+        )
+
+        @pl.when(i == pl.num_programs(0) - 1)
+        def _():
+            out_ref[...] = acc[...].astype(out_ref.dtype)
+
+    return pl.pallas_call(
+        body,
+        out_shape=jax.ShapeDtypeStruct((tall, quarter), pairs.dtype),
+        grid_spec=pltpu.PrefetchScalarGridSpec(
+            num_scalar_prefetch=1,
+            grid=(cols // step,),
+            in_specs=[
+                pl.BlockSpec((tall, step), lambda i, own_ref: (0, i)),
+                pl.BlockSpec((quarter, step), lambda i, own_ref: (own_ref[0] ^ k, i)),
+            ],
+            out_specs=pl.BlockSpec((tall, quarter), lambda i, own_ref: (0, 0)),
+            scratch_shapes=[pltpu.VMEM((tall, quarter), jnp.float32)],
+        ),
+        compiler_params=pltpu.CompilerParams(vmem_limit_bytes=16 * 1024 * 1024),
+        cost_estimate=pl.CostEstimate(
+            flops=2 * tall * quarter * cols, transcendentals=0, bytes_accessed=14_000_000
+        ),
+        name="tower_piece",
+    )(own, pairs, cotangent)
+
+
 def owner_step(parts, selected, squeezed, table, slot_index, w_ex, w_ext, w_sq, w_sqt, slots):
     tables, span, samples = parts.shape
     count, width, _ = selected.shape
@@ -449,12 +493,12 @@
     cut = jnp.concatenate([cut, jnp.zeros((1, unit, quarter), bf16)], axis=0)
     cut = jnp.take(cut, jnp.asarray(plan["pick"])[here], axis=0, mode="clip")
     cut = cut.reshape(plane, depth * width, quarter)
-    cut = trade([cut[k] for k in range(plane)], "table", tables)
-    cut = jnp.concatenate(cut, axis=0)
 
     sent = pack_rows(received, squeeze_rows, slot_index, table)
     sent, cut = lax.optimization_barrier((sent, cut))
     got = lax.all_to_all(sent, "table", split_axis=0, concat_axis=0, tiled=True)
+    cut = trade([cut[k] for k in range(plane)], "table", tables)
+    cut = jnp.concatenate(cut, axis=0)
     pieces = trade([cut] * subs, "sub", subs)
 
     cotangent = lax.all_gather(tower_cotangent, "table", axis=1, tiled=True)
@@ -484,14 +528,34 @@
     )
     parts = lax.all_to_all(part, "table", split_axis=0, concat_axis=0, tiled=True)
 
-    total = lax.dot_general(
-        pairs, cotangent, (((1,), (1,)), ((), ())), preferred_element_type=f32
-    )
-    total = jnp.moveaxis(total.astype(bf16).reshape(-1, subs, quarter), 1, 0)
-    total = xor_order(total, "sub")
-    total = trade([total[k] for k in range(subs)], "sub", subs)
+    own_now = own_sub[None]
+    total = [None] * subs
+    for k in sorted(range(subs), key=lambda k: (k == 0, k != 2, k)):
+        piece = tower_piece(own_now, pairs, cotangent, subs, k)
+        own_now, piece = lax.optimization_barrier((own_now, piece))
+        total[k] = swap(piece, "sub", subs, k) if k else piece
+    d_excite, d_squeeze, d_bilinear, _ = lax.optimization_barrier(
+        (d_excite, d_squeeze, d_bilinear, own_now)
+    )
     total = sum(x.astype(f32) for x in total) * (1.0 / total_samples)
-    total = total.astype(bf16).reshape(plane, depth * width, quarter)
+    bundled = [x.T.reshape(w_squeeze.shape[0], count // 8, 8 * width).transpose(1, 0, 2) for x in (xh, xl)]
+    placed = owner_step(
+        parts,
+        selected,
+        squeeze_rows,
+        table,
+        slot_index,
+        jnp.concatenate([xh, xl, xh], axis=1),
+        jnp.stack(bundled, axis=1),
+        w_sq,
+        jnp.concatenate([s1, s1, s2], axis=0).T,
+        per_owner * tables,
+    )
+    total = total.astype(bf16)
+    placed, total = lax.optimization_barrier((placed, total))
+    placed = placed.reshape(per_owner * tables, 1, 1, width, samples)
+    row_grads = lax.all_to_all(placed, "table", split_axis=0, concat_axis=1, tiled=True)
+    total = total.reshape(plane, depth * width, quarter)
     total = trade([total[k] for k in range(plane)], "table", tables)
     total = jnp.concatenate(total, axis=0).reshape(-1, unit, quarter)
     total = jnp.take(total, jnp.asarray(plan["back"])[here], axis=0, mode="clip")
@@ -528,21 +592,6 @@
     g_squeeze = small[ends[0] : ends[1]].reshape(w_squeeze.shape)
     g_bilinear = small[ends[1] : ends[2]].reshape(w_bilinear.shape)
 
-    bundled = [x.T.reshape(hidden_units, count // 8, 8 * width).transpose(1, 0, 2) for x in (xh, xl)]
-    placed = owner_step(
-        parts,
-        selected,
-        squeeze_rows,
-        table,
-        slot_index,
-        jnp.concatenate([xh, xl, xh], axis=1),
-        jnp.stack(bundled, axis=1),
-        w_sq,
-        jnp.concatenate([s1, s1, s2], axis=0).T,
-        per_owner * tables,
-    )
-    placed = placed.reshape(per_owner * tables, 1, 1, width, samples)
-    row_grads = lax.all_to_all(placed, "table", split_axis=0, concat_axis=1, tiled=True)
     return (row_grads, weight_grad, g_squeeze, g_excite, g_bilinear)
 
 

time: 326 us -> 350 us (1.074)
  waiting for transfers between devices: 101 us -> 126 us
  Pallas kernels: 49 us -> 71.1 us
  matrix products: 18.6 us -> 1.97 us
  local copies, waits for them, and re-layouts: 54.3 us -> 46.9 us
    ppermute x33, waiting for transfers between devices: 85.5 us -> 116 us  [swap(): return lax.ppermute(value, axis, [(a, a ^ k) for a in range(size)])]
    pallas_call x0 -> x4, Pallas kernels: none -> 22.1 us  [tower_piece(): pl.pallas_call(body, out_shape=jax.ShapeDtypeStruct((tall, quarter), pair...]
    dot_general x1 -> x0, matrix products: 17.4 us -> none  [on_device(): lax.dot_general(pairs, cotangent, (((1,), (1,)), ((), ())), preferred_ele...]
    all_gather x1, waiting for transfers between devices: 14.4 us -> 0.01 us  [on_device(): cotangent = lax.all_gather(tower_cotangent, 'table', axis=1, tiled=True)]
    all_to_all x1, waiting for transfers between devices: 0.01 us -> 10.2 us  [on_device(): lax.all_to_all(rotated, 'table', split_axis=1, concat_axis=0, tiled=True)]
    unnamed x76 -> x88, local copies, waits for them, and re-layouts: 18.4 us -> 23.1 us
    gather x5 -> x4, local copies, waits for them, and re-layouts: 6.4 us -> 2.58 us  [xor_order(): jnp.take(blocks, own ^ jnp.arange(blocks.shape[0], dtype=jnp.int32), axis...]
  transfers between devices with their start and end apart: 38 -> 38, of which waited for: 18 -> 17; matrix products, arithmetic and copies ran while one was open for 21% -> 11% of each run, Pallas kernels for 7% -> 13%
where the time goes in v1:
time: 350 us; the launch traced here: 345 us
  waiting for transfers between devices  126 us (36%)
  starting transfers between devices  74.3 us (21%)
  Pallas kernels  71.1 us (20%)
  local copies, waits for them, and re-layouts  46.9 us (13%)
  between operations  14.9 us (4%)
  other arithmetic  9.11 us (3%)
    ppermute x33, waiting for transfers between devices, swap(): return lax.ppermute(value, axis, [(a, a ^ k) for a in range(size)])  116 us
    ppermute x33, starting transfers between devices, swap(): return lax.ppermute(value, axis, [(a, a ^ k) for a in range(size)])  46.2 us
    pallas_call x1, Pallas kernels, pair_step(): pl.pallas_call(body, out_shape=(jax.ShapeDtypeStruct((slots * width, tabl...  26.1 us
    unnamed x88, local copies, waits for them, and re-layouts  23.1 us
    pallas_call x4, Pallas kernels, tower_piece(): pl.pallas_call(body, out_shape=jax.ShapeDtypeStruct((tall, quarter), pair...  22.1 us
    pallas_call x1, Pallas kernels, tower_pairs(): pl.pallas_call(body, out_shape=jax.ShapeDtypeStruct((tall, cols), cotange...  14.4 us
    all_to_all x1, waiting for transfers between devices, on_device(): lax.all_to_all(rotated, 'table', split_axis=1, concat_axis=0, tiled=True)  10.2 us
    all_to_all x1, starting transfers between devices, on_device(): lax.all_to_all(rotated, 'table', split_axis=1, concat_axis=0, tiled=True)  8.47 us
  transfers between devices with their start and end apart: 38, of which 17 were waited for; matrix products, arithmetic and copies ran while one was open for 11% of the time, Pallas kernels for 13%

profile of v1, /device:TPU:10, one launch (start us, length us, event | category | flops | bytes accessed | tf_op | source)
XLA Modules:
  0.0 344.7 jit_solution(17668901285394430655)
XLA Ops:
  8.3 1.0 fusion
  11.0 2.6 collective-permute-start.1
  14.9 8.5 %all-to-all-start = ((bf16[3,32,1,32,128]{4,3,0,2,1:T(8,128)(2,1)}), bf16[3,32,1,32,128]{4,3,0,2,1:T(8,128)(2,1)S(1)}, u32[]{:S(2)}, u32[]{:S(2)}) async-start(bf16[3,32,1,32,128]{4,3,0,2,1:T(8,128)(2,1)} %copy.149), calls=%async_computation | async-start | bytes 1572864 | tf_op jit(solution)/shard_map/all_to_all | solution.py:480
  29.0 10.2 %all-to-all-done = bf16[3,32,1,32,128]{4,3,0,2,1:T(8,128)(2,1)S(1)} async-done(((bf16[3,32,1,32,128]{4,3,0,2,1:T(8,128)(2,1)}), bf16[3,32,1,32,128]{4,3,0,2,1:T(8,128)(2,1)S(1)}, u32[]{:S(2)}, u32[]{:S(2)}) %all-to-all-start) | async-done | bytes 786464 | tf_op jit(solution)/shard_map/all_to_all | solution.py:480
  40.6 4.4 %pack_rows.1 = bf16[32,464,128]{2,1,0:T(8,128)(2,1)} custom-call(s32[48]{0:T(128)} %copy-done.19, s32[416]{0:T(512)} %constant.52.clone.table_ref, bf16[96,32,128]{2,1,0:T(8,128)(2,1)} %bitcast.150, bf16[48,128]{1,0:T(8,128)(2,1)} %bitcast.147), custom_call_target="tpu_custom_call" | custom-call | tf_op jit(solution)/shard_map/pack_rows/pallas_call | solution.py:148
  44.9 6.3 %all-to-all-start.1 = ((bf16[32,464,128]{2,1,0:T(8,128)(2,1)}), bf16[32,464,128]{2,1,0:T(8,128)(2,1)}, u32[]{:S(2)}, u32[]{:S(2)}) async-start(bf16[32,464,128]{2,1,0:T(8,128)(2,1)} %pack_rows.1), calls=%async_computation.1 | async-start | bytes 7602176 | tf_op jit(solution)/shard_map/all_to_all | solution.py:499
  52.4 1.3 collective-permute-start.5
  53.7 2.1 collective-permute-start.6
  55.8 1.2 collective-permute-start.7
  57.0 1.5 collective-permute-start.8
  58.4 47.4 %collective-permute-done.4 = bf16[160,256]{1,0:T(8,128)(2,1)S(1)} collective-permute-done((bf16[160,256]{1,0:T(8,128)(2,1)S(1)}, bf16[160,256]{1,0:T(8,128)(2,1)S(1)}, u32[]{:S(2)}, u32[]{:S(2)}) %collective-permute-start.4) | collective-permute-done | bytes 81952 | tf_op jit(solution)/shard_map/ppermute | solution.py:115
  105.8 2.3 collective-permute-start.9
  108.6 6.6 %collective-permute-done.6 = bf16[160,256]{1,0:T(8,128)(2,1)S(1)} collective-permute-done((bf16[160,256]{1,0:T(8,128)(2,1)S(1)}, bf16[160,256]{1,0:T(8,128)(2,1)S(1)}, u32[]{:S(2)}, u32[]{:S(2)}) %collective-permute-start.6) | collective-permute-done | bytes 81952 | tf_op jit(solution)/shard_map/ppermute | solution.py:115
  115.1 2.6 collective-permute-done.7
  117.8 1.2 collective-permute-start.10
  118.9 2.2 collective-permute-start.11
  123.4 12.1 %collective-permute-done.10.refs_1_ = bf16[1280,256]{1,0:T(8,128)(2,1)S(1)} collective-permute-done((bf16[1280,256]{1,0:T(8,128)(2,1)S(1)}, bf16[1280,256]{1,0:T(8,128)(2,1)S(1)}, u32[]{:S(2)}, u32[]{:S(2)}) %collective-permute-start.10) | collective-permute-done | bytes 655392 | tf_op jit(solution)/shard_map/ppermute | solution.py:115
  135.5 14.8 %collective-permute-done.11.refs_2_ = bf16[1280,256]{1,0:T(8,128)(2,1)S(1)} collective-permute-done((bf16[1280,256]{1,0:T(8,128)(2,1)S(1)}, bf16[1280,256]{1,0:T(8,128)(2,1)S(1)}, u32[]{:S(2)}, u32[]{:S(2)}) %collective-permute-start.11) | collective-permute-done | bytes 655392 | tf_op jit(solution)/shard_map/ppermute | solution.py:115
  150.3 1.4 collective-permute-done.12.refs_3_
  152.5 3.4 copy-done.3
  155.9 1.1 copy-done.22
  157.0 14.4 %tower_pairs.1.pg_ref = bf16[1280,4096]{1,0:T(8,128)(2,1)} custom-call(s32[1]{0:T(128)} %bitcast.24.own_ref, bf16[1280,256]{1,0:T(8,128)(2,1)S(1)} %constant_dynamic-update-slice_fusion.refs_0_, bf16[1280,256]{1,0:T(8,128)(2,1)S(1)} %collective-permute-done.10.refs_1_, bf16[1280,256]{1,0:T(8,128)(2,1)S(1)} %collective-permute-done.11.refs_2_, ...), custom_call_target="tpu_custom_call" | custom-call | flops 10737418240 | bytes 30000000 | tf_op jit(solution)/shard_map/tower_pairs/pallas_call | solution.py:186
  171.5 26.1 %pair_step.1 = (bf16[1280,4096]{1,0:T(8,128)(2,1)}, bf16[32,416,128]{2,1,0:T(8,128)(2,1)S(1)}, f32[416,224]{1,0:T(8,128)S(1)}, f32[32,416]{1,0:T(8,128)S(1)}, f32[32,48]{1,0:T(8,128)S(1)}) custom-call(s32[40]{0:T(128)S(1)} %get-tuple-element.106.left_ref, s32[40]{0:T(128)S(1)} %get-tuple-element.107.right_ref, bf16[32,464,128]{2,1,0:T(8,128)(2,1)} %all-to-all-done.1.got_ref, ...), custom_call_target="tpu_custom_call" | custom-call | tf_op jit(solution)/shard_map/pair_step/pallas_call | solution.py:427
  197.6 1.8 copy-done.5
  200.8 6.8 %all-to-all-start.2 = ((bf16[32,416,128]{2,1,0:T(8,128)(2,1)}), bf16[32,416,128]{2,1,0:T(8,128)(2,1)S(1)}, u32[]{:S(2)}, u32[]{:S(2)}) async-start(bf16[32,416,128]{2,1,0:T(8,128)(2,1)} %copy-done.5), calls=%async_computation.2 | async-start | bytes 6815744 | tf_op jit(solution)/shard_map/all_to_all | solution.py:529
  208.2 1.8 copy.166.wex_ref
  210.9 1.4 slice_add_fusion
  212.3 1.5 reshape.141
  213.8 1.7 copy.170
  215.5 1.7 reshape.142
  218.8 1.6 slice_add_fusion.1
  222.4 4.0 %copy-done.2 = bf16[1280,4096]{1,0:T(8,128)(2,1)S(1)} copy-done((bf16[1280,4096]{1,0:T(8,128)(2,1)S(1)}, bf16[1280,4096]{1,0:T(8,128)(2,1)}, u32[]{:S(2)}) %copy-start.2) | copy-done | bytes 10485784
  226.3 3.4 copy-done.4
  229.7 5.5 %tower_piece.4 = bf16[1280,256]{1,0:T(8,128)(2,1)S(1)} custom-call(s32[1]{0:T(128)} %bitcast.24.own_ref, bf16[1280,4096]{1,0:T(8,128)(2,1)S(1)} %copy-done.2, bf16[1024,4096]{1,0:T(8,128)(2,1)S(1)} %copy-done.4), custom_call_target="tpu_custom_call" | custom-call | flops 2684354560 | bytes 14000000 | tf_op jit(solution)/shard_map/tower_piece/pallas_call | solution.py:230
  235.3 5.5 %tower_piece.5 = bf16[1280,256]{1,0:T(8,128)(2,1)S(1)} custom-call(s32[1]{0:T(128)} %bitcast.24.own_ref, bf16[1280,4096]{1,0:T(8,128)(2,1)S(1)} %copy-done.2, bf16[1024,4096]{1,0:T(8,128)(2,1)S(1)} %copy-done.4), custom_call_target="tpu_custom_call" | custom-call | flops 2684354560 | bytes 14000000 | tf_op jit(solution)/shard_map/tower_piece/pallas_call | solution.py:230
  241.3 5.5 %tower_piece.6 = bf16[1280,256]{1,0:T(8,128)(2,1)S(1)} custom-call(s32[1]{0:T(128)} %bitcast.24.own_ref, bf16[1280,4096]{1,0:T(8,128)(2,1)S(1)} %copy-done.2, bf16[1024,4096]{1,0:T(8,128)(2,1)S(1)} %copy-done.4), custom_call_target="tpu_custom_call" | custom-call | flops 2684354560 | bytes 14000000 | tf_op jit(solution)/shard_map/tower_piece/pallas_call | solution.py:230
  247.5 3.3 collective-permute-start.13
  250.7 1.8 collective-permute-start.14
  252.5 2.6 collective-permute-start.28
  255.2 3.6 %collective-permute-done.28 = f32[208,128]{1,0:T(8,128)S(1)} collective-permute-done((f32[208,128]{1,0:T(8,128)S(1)}, f32[208,128]{1,0:T(8,128)S(1)}, u32[]{:S(2)}, u32[]{:S(2)}) %collective-permute-start.28) | collective-permute-done | bytes 106528 | tf_op jit(solution)/shard_map/ppermute | solution.py:115
  258.8 1.7 collective-permute-start.29
  261.3 2.4 collective-permute-done.29
  263.6 3.2 collective-permute-start.30
  266.9 5.5 %tower_piece.7 = bf16[1280,256]{1,0:T(8,128)(2,1)S(1)} custom-call(s32[1]{0:T(128)} %bitcast.24.own_ref, bf16[1280,4096]{1,0:T(8,128)(2,1)S(1)} %copy-done.2, bf16[1024,4096]{1,0:T(8,128)(2,1)S(1)} %copy-done.4), custom_call_target="tpu_custom_call" | custom-call | flops 2684354560 | bytes 14000000 | tf_op jit(solution)/shard_map/tower_piece/pallas_call | solution.py:230
  273.1 2.6 collective-permute-start.31
  275.7 6.4 %collective-permute-done.14 = bf16[1280,256]{1,0:T(8,128)(2,1)S(1)} collective-permute-done((bf16[1280,256]{1,0:T(8,128)(2,1)S(1)}, bf16[1280,256]{1,0:T(8,128)(2,1)S(1)}, u32[]{:S(2)}, u32[]{:S(2)}) %collective-permute-start.14) | collective-permute-done | bytes 655392 | tf_op jit(solution)/shard_map/ppermute | solution.py:115
  282.1 1.2 multiply_convert_fusion.1
  283.4 1.0 copy-done.8
  284.4 1.0 copy-done.9
  286.3 4.0 %owner_step.1 = bf16[96,32,128]{2,1,0:T(8,128)(2,1)S(1)} custom-call(s32[416]{0:T(512)S(1)} %copy-done.18, s32[48]{0:T(128)S(1)} %copy-done.20, bf16[32,416,128]{2,1,0:T(8,128)(2,1)S(1)} %all-to-all-done.2.parts_ref, bf16[48,32,128]{2,1,0:T(8,128)(2,1)S(1)} %copy-done.8, bf16[48,128]{1,0:T(8,128)(2,1)S(1)} %bitcast.148, bf16[256,256]{1,0:T(8,128)(2,1)S(1)} %copy-done.12, ...), custom_call_target="tpu_custom_call" | custom-call | tf_op jit(solution)/shard_map/owner_step/pallas_call | solution.py:302
  290.5 1.1 add.111
  291.6 1.8 collective-permute-start.32
  293.4 1.6 collective-permute-start.17
  295.1 2.3 collective-permute-start.19
  297.4 6.5 %all-to-all-start.3 = ((bf16[96,1,1,32,128]{4,3,2,1,0:T(8,128)(2,1)}), bf16[96,1,1,32,128]{4,3,2,1,0:T(8,128)(2,1)S(1)}, u32[]{:S(2)}, u32[]{:S(2)}) async-start(bf16[96,1,1,32,128]{4,3,2,1,0:T(8,128)(2,1)} %bitcast.145), calls=%async_computation.3 | async-start | bytes 1572864 | tf_op jit(solution)/shard_map/all_to_all | solution.py:557
  303.9 1.9 collective-permute-start.20
  305.9 1.8 collective-permute-start.22
  307.7 8.9 %collective-permute-done.20 = bf16[160,256]{1,0:T(8,128)(2,1)S(1)} collective-permute-done((bf16[160,256]{1,0:T(8,128)(2,1)S(1)}, bf16[160,256]{1,0:T(8,128)(2,1)S(1)}, u32[]{:S(2)}, u32[]{:S(2)}) %collective-permute-start.20) | collective-permute-done | bytes 81952 | tf_op jit(solution)/shard_map/ppermute | solution.py:115
  316.7 2.3 collective-permute-done.21
  321.2 1.3 collective-permute-start.23
  322.5 2.6 collective-permute-start.24
  328.0 4.5 %collective-permute-done.24 = bf16[282,256]{1,0:T(8,128)(2,1)S(1)} collective-permute-done((bf16[282,256]{1,0:T(8,128)(2,1)S(1)}, bf16[282,256]{1,0:T(8,128)(2,1)S(1)}, u32[]{:S(2)}, u32[]{:S(2)}) %collective-permute-start.24) | collective-permute-done | bytes 144416 | tf_op jit(solution)/shard_map/ppermute | solution.py:115
  332.5 1.4 collective-permute-done.25
  335.7 1.2 copy.176
  (200 shorter events, 33.5 us)
Async XLA Ops:
  7.2 2.2 copy-start.26
  7.2 145.3 %all-gather.2.cloned.1.call-start = ((), (), s32[]{:S(2)}) async-start(), calls=%async_computation.4 | async-start | bytes 8650752 | tf_op jit(solution)/shard_map/all_gather | solution.py:504
  9.8 17.7 %copy-start.32 = (s32[1024]{0:T(1024)}, s32[1024]{0:T(1024)S(1)}, u32[]{:S(2)}) copy-start(s32[1024]{0:T(1024)S(1)} %pad_clamp_fusion.3) | copy-start | bytes 12292
  10.4 16.9 %collective-permute-start = (bf16[282,256]{1,0:T(8,128)(2,1)S(1)}, bf16[282,256]{1,0:T(8,128)(2,1)S(1)}, u32[]{:S(2)}, u32[]{:S(2)}) collective-permute-start(bf16[282,256]{1,0:T(8,128)(2,1)S(1)} %get-tuple-element.100), channel_id=1, source_target_pairs={{0,1},{1,0},{2,3},{3,2},{4,5},{5,4},{6,7},{7,6},{8,9},{9,8},{10,11... | collective-permute-start | bytes 433160 | tf_op jit(solution)/shard_map/ppermute | solution.py:115
  11.0 16.4 %collective-permute-start.1 = (bf16[282,256]{1,0:T(8,128)(2,1)S(1)}, bf16[282,256]{1,0:T(8,128)(2,1)S(1)}, u32[]{:S(2)}, u32[]{:S(2)}) collective-permute-start(bf16[282,256]{1,0:T(8,128)(2,1)S(1)} %get-tuple-element.99), channel_id=1, source_target_pairs={{0,2},{1,3},{2,0},{3,1},{4,6},{5,7},{6,4},{7,5},{8,10},{9,11},{10,... | collective-permute-start | bytes 433160 | tf_op jit(solution)/shard_map/ppermute | solution.py:115
  13.5 9.9 %copy-start.31 = (f32[16,48]{1,0:T(8,128)S(1)}, f32[16,48]{1,0:T(8,128)}, u32[]{:S(2)}) copy-start(f32[16,48]{1,0:T(8,128)} %param.22) | copy-start | bytes 9220
  13.5 11.5 %copy-start.33 = (s32[48]{0:T(128)S(1)}, s32[48]{0:T(128)}, u32[]{:S(2)}) copy-start(s32[48]{0:T(128)} %param.21) | copy-start | bytes 580
  13.6 11.7 %copy-start.29 = (f32[1536,16]{0,1:T(8,128)S(1)}, f32[1536,16]{0,1:T(8,128)}, u32[]{:S(2)}) copy-start(f32[1536,16]{0,1:T(8,128)} %param.23) | copy-start | bytes 294916
  13.6 13.8 %collective-permute-start.2 = (bf16[282,256]{1,0:T(8,128)(2,1)S(1)}, bf16[282,256]{1,0:T(8,128)(2,1)S(1)}, u32[]{:S(2)}, u32[]{:S(2)}) collective-permute-start(bf16[282,256]{1,0:T(8,128)(2,1)S(1)} %get-tuple-element.101), channel_id=1, source_target_pairs={{0,3},{1,2},{2,1},{3,0},{4,7},{5,6},{6,5},{7,4},{8,11},{9,10},{10,... | collective-permute-start | bytes 433160 | tf_op jit(solution)/shard_map/ppermute | solution.py:115
  14.9 24.3 %all-to-all-start = ((bf16[3,32,1,32,128]{4,3,0,2,1:T(8,128)(2,1)}), bf16[3,32,1,32,128]{4,3,0,2,1:T(8,128)(2,1)S(1)}, u32[]{:S(2)}, u32[]{:S(2)}) async-start(bf16[3,32,1,32,128]{4,3,0,2,1:T(8,128)(2,1)} %copy.149), calls=%async_computation | async-start | bytes 1572864 | tf_op jit(solution)/shard_map/all_to_all | solution.py:480
  25.2 2.3 copy-start.19
  25.2 2.2 copy-start.27
  39.2 1.3 copy-start.23
  39.9 5.1 %copy-start.7 = (bf16[48,32,128]{2,1,0:T(8,128)(2,1)}, bf16[48,32,128]{2,1,0:T(8,128)(2,1)S(1)}, u32[]{:S(2)}) copy-start(bf16[48,32,128]{2,1,0:T(8,128)(2,1)S(1)} %gather_fusion) | copy-start | bytes 1179652
  44.9 6.6 %copy-start.30 = (f32[32,32]{1,0:T(8,128)S(1)}, f32[32,32]{1,0:T(8,128)}, u32[]{:S(2)}) copy-start(f32[32,32]{1,0:T(8,128)} %param.24) | copy-start | bytes 12292
  44.9 126.5 %all-to-all-start.1 = ((bf16[32,464,128]{2,1,0:T(8,128)(2,1)}), bf16[32,464,128]{2,1,0:T(8,128)(2,1)}, u32[]{:S(2)}, u32[]{:S(2)}) async-start(bf16[32,464,128]{2,1,0:T(8,128)(2,1)} %pack_rows.1), calls=%async_computation.1 | async-start | bytes 7602176 | tf_op jit(solution)/shard_map/all_to_all | solution.py:499
  51.7 5.2 %collective-permute-start.3 = (bf16[160,256]{1,0:T(8,128)(2,1)S(1)}, bf16[160,256]{1,0:T(8,128)(2,1)S(1)}, u32[]{:S(2)}, u32[]{:S(2)}) collective-permute-start(bf16[160,256]{1,0:T(8,128)(2,1)S(1)} %get-tuple-element.93), channel_id=1, source_target_pairs={{0,4},{4,0},{8,12},{12,8},{16,20},{20,16},{24,28},{28,24},{32,36},... | collective-permute-start | bytes 245768 | tf_op jit(solution)/shard_map/ppermute | solution.py:115
  51.9 53.9 %collective-permute-start.4 = (bf16[160,256]{1,0:T(8,128)(2,1)S(1)}, bf16[160,256]{1,0:T(8,128)(2,1)S(1)}, u32[]{:S(2)}, u32[]{:S(2)}) collective-permute-start(bf16[160,256]{1,0:T(8,128)(2,1)S(1)} %get-tuple-element.92), channel_id=1, source_target_pairs={{0,8},{4,12},{8,0},{12,4},{16,24},{20,28},{24,16},{28,20},{32,40},... | collective-permute-start | bytes 245768 | tf_op jit(solution)/shard_map/ppermute | solution.py:115
  52.4 56.2 %collective-permute-start.5 = (bf16[160,256]{1,0:T(8,128)(2,1)S(1)}, bf16[160,256]{1,0:T(8,128)(2,1)S(1)}, u32[]{:S(2)}, u32[]{:S(2)}) collective-permute-start(bf16[160,256]{1,0:T(8,128)(2,1)S(1)} %get-tuple-element.91), channel_id=1, source_target_pairs={{0,12},{4,8},{8,4},{12,0},{16,28},{20,24},{24,20},{28,16},{32,44},... | collective-permute-start | bytes 245768 | tf_op jit(solution)/shard_map/ppermute | solution.py:115
  53.7 61.5 %collective-permute-start.6 = (bf16[160,256]{1,0:T(8,128)(2,1)S(1)}, bf16[160,256]{1,0:T(8,128)(2,1)S(1)}, u32[]{:S(2)}, u32[]{:S(2)}) collective-permute-start(bf16[160,256]{1,0:T(8,128)(2,1)S(1)} %get-tuple-element.90), channel_id=1, source_target_pairs={{0,16},{4,20},{8,24},{12,28},{16,0},{20,4},{24,8},{28,12},{32,48},... | collective-permute-start | bytes 245768 | tf_op jit(solution)/shard_map/ppermute | solution.py:115
  55.8 62.0 %collective-permute-start.7 = (bf16[160,256]{1,0:T(8,128)(2,1)S(1)}, bf16[160,256]{1,0:T(8,128)(2,1)S(1)}, u32[]{:S(2)}, u32[]{:S(2)}) collective-permute-start(bf16[160,256]{1,0:T(8,128)(2,1)S(1)} %get-tuple-element.89), channel_id=1, source_target_pairs={{0,20},{4,16},{8,28},{12,24},{16,4},{20,0},{24,12},{28,8},{32,52},... | collective-permute-start | bytes 245768 | tf_op jit(solution)/shard_map/ppermute | solution.py:115
  57.0 60.8 %collective-permute-start.8 = (bf16[160,256]{1,0:T(8,128)(2,1)S(1)}, bf16[160,256]{1,0:T(8,128)(2,1)S(1)}, u32[]{:S(2)}, u32[]{:S(2)}) collective-permute-start(bf16[160,256]{1,0:T(8,128)(2,1)S(1)} %get-tuple-element.88), channel_id=1, source_target_pairs={{0,24},{4,28},{8,16},{12,20},{16,8},{20,12},{24,0},{28,4},{32,56},... | collective-permute-start | bytes 245768 | tf_op jit(solution)/shard_map/ppermute | solution.py:115
  105.8 11.9 %collective-permute-start.9 = (bf16[160,256]{1,0:T(8,128)(2,1)S(1)}, bf16[160,256]{1,0:T(8,128)(2,1)S(1)}, u32[]{:S(2)}, u32[]{:S(2)}) collective-permute-start(bf16[160,256]{1,0:T(8,128)(2,1)S(1)} %get-tuple-element.87), channel_id=1, source_target_pairs={{0,28},{4,24},{8,20},{12,16},{16,12},{20,8},{24,4},{28,0},{32,60},... | collective-permute-start | bytes 245768 | tf_op jit(solution)/shard_map/ppermute | solution.py:115
  117.8 17.7 %collective-permute-start.10 = (bf16[1280,256]{1,0:T(8,128)(2,1)S(1)}, bf16[1280,256]{1,0:T(8,128)(2,1)S(1)}, u32[]{:S(2)}, u32[]{:S(2)}) collective-permute-start(bf16[1280,256]{1,0:T(8,128)(2,1)S(1)} %constant_dynamic-update-slice_fusion.refs_0_), channel_id=1, source_target_pairs={{0,1},{1,0},{2,3},{3,2},{4,5},{5,4},{6,7},{7,6},{8,9},{9,8},{10,11... | collective-permute-start | bytes 1966088 | tf_op jit(solution)/shard_map/ppermute | solution.py:115
  118.9 31.4 %collective-permute-start.11 = (bf16[1280,256]{1,0:T(8,128)(2,1)S(1)}, bf16[1280,256]{1,0:T(8,128)(2,1)S(1)}, u32[]{:S(2)}, u32[]{:S(2)}) collective-permute-start(bf16[1280,256]{1,0:T(8,128)(2,1)S(1)} %constant_dynamic-update-slice_fusion.refs_0_), channel_id=1, source_target_pairs={{0,2},{1,3},{2,0},{3,1},{4,6},{5,7},{6,4},{7,5},{8,10},{9,11},{10,... | collective-permute-start | bytes 1966088 | tf_op jit(solution)/shard_map/ppermute | solution.py:115
  121.1 30.5 %collective-permute-start.12 = (bf16[1280,256]{1,0:T(8,128)(2,1)S(1)}, bf16[1280,256]{1,0:T(8,128)(2,1)S(1)}, u32[]{:S(2)}, u32[]{:S(2)}) collective-permute-start(bf16[1280,256]{1,0:T(8,128)(2,1)S(1)} %constant_dynamic-update-slice_fusion.refs_0_), channel_id=1, source_target_pairs={{0,3},{1,2},{2,1},{3,0},{4,7},{5,6},{6,5},{7,4},{8,11},{9,10},{10,... | collective-permute-start | bytes 1966088 | tf_op jit(solution)/shard_map/ppermute | solution.py:115
  152.5 3.4 copy-start.3
  157.0 14.5 %copy-start.10 = (f32[416,224]{1,0:T(8,128)S(1)}, f32[416,224]{1,0:T(8,128)}, u32[]{:S(2)}) copy-start(f32[416,224]{1,0:T(8,128)} %constant.60.clone.mask_ref) | copy-start | bytes 1118212
  157.0 14.5 %copy-start.11 = (bf16[416,224]{1,0:T(8,128)(2,1)S(1)}, bf16[416,224]{1,0:T(8,128)(2,1)}, u32[]{:S(2)}) copy-start(bf16[416,224]{1,0:T(8,128)(2,1)} %constant.57.clone.hd_ref) | copy-start | bytes 559108
  157.0 14.5 %copy-start.14 = (bf16[416,32]{1,0:T(8,128)(2,1)S(1)}, bf16[416,32]{1,0:T(8,128)(2,1)}, u32[]{:S(2)}) copy-start(bf16[416,32]{1,0:T(8,128)(2,1)} %constant.58.clone.rep_ref) | copy-start | bytes 79876
  157.0 14.5 %copy-start.17 = (bf16[32,224]{1,0:T(8,128)(2,1)S(1)}, bf16[32,224]{1,0:T(8,128)(2,1)}, u32[]{:S(2)}) copy-start(bf16[32,224]{1,0:T(8,128)(2,1)} %constant.59.clone.rept_ref) | copy-start | bytes 43012
  197.6 1.8 copy-start.5
  200.8 82.6 %all-to-all-start.2 = ((bf16[32,416,128]{2,1,0:T(8,128)(2,1)}), bf16[32,416,128]{2,1,0:T(8,128)(2,1)S(1)}, u32[]{:S(2)}, u32[]{:S(2)}) async-start(bf16[32,416,128]{2,1,0:T(8,128)(2,1)} %copy-done.5), calls=%async_computation.2 | async-start | bytes 6815744 | tf_op jit(solution)/shard_map/all_to_all | solution.py:529
  222.2 18.6 %collective-permute-start.26 = (f32[208,128]{1,0:T(8,128)S(1)}, f32[208,128]{1,0:T(8,128)S(1)}, u32[]{:S(2)}, u32[]{:S(2)}) collective-permute-start(f32[208,128]{1,0:T(8,128)S(1)} %fusion.2), channel_id=1, source_target_pairs={{0,4},{4,0},{8,12},{12,8},{16,20},{20,16},{24,28},{28,24},{32,36},... | collective-permute-start | bytes 319496 | tf_op jit(solution)/shard_map/ppermute | solution.py:115
  222.4 4.0 %copy-start.2 = (bf16[1280,4096]{1,0:T(8,128)(2,1)S(1)}, bf16[1280,4096]{1,0:T(8,128)(2,1)}, u32[]{:S(2)}) copy-start(bf16[1280,4096]{1,0:T(8,128)(2,1)} %get-tuple-element.31.pairs_ref) | copy-start | bytes 31457284
  226.3 3.4 copy-start.4
  235.2 5.6 %copy-start.25 = (f32[6,4,8,128]{3,1,2,0:T(4,128)S(1)}, f32[6,4,8,128]{3,1,2,0:T(4,128)}, u32[]{:S(2)}) copy-start(f32[6,4,8,128]{3,1,2,0:T(4,128)} %copy.177) | copy-start | bytes 294916
  240.9 14.3 %copy-start.28 = (bf16[16,48]{0,1:T(8,128)(2,1)S(1)}, bf16[16,48]{0,1:T(8,128)(2,1)}, u32[]{:S(2)}) copy-start(bf16[16,48]{0,1:T(8,128)(2,1)} %copy-done.27) | copy-start | bytes 4612
  240.9 11.7 %collective-permute-start.27 = (f32[208,128]{1,0:T(8,128)S(1)}, f32[208,128]{1,0:T(8,128)S(1)}, u32[]{:S(2)}, u32[]{:S(2)}) collective-permute-start(f32[208,128]{1,0:T(8,128)S(1)} %fusion.16), channel_id=1, source_target_pairs={{0,8},{4,12},{8,0},{12,4},{16,24},{20,28},{24,16},{28,20},{32,40},... | collective-permute-start | bytes 319496 | tf_op jit(solution)/shard_map/ppermute | solution.py:115
  246.9 28.8 %collective-permute-start.15 = (bf16[1280,256]{1,0:T(8,128)(2,1)S(1)}, bf16[1280,256]{1,0:T(8,128)(2,1)S(1)}, u32[]{:S(2)}, u32[]{:S(2)}) collective-permute-start(bf16[1280,256]{1,0:T(8,128)(2,1)S(1)} %tower_piece.6), channel_id=1, source_target_pairs={{0,3},{1,2},{2,1},{3,0},{4,7},{5,6},{6,5},{7,4},{8,11},{9,10},{10,... | collective-permute-start | bytes 1966088 | tf_op jit(solution)/shard_map/ppermute | solution.py:115
  247.5 28.3 %collective-permute-start.13 = (bf16[1280,256]{1,0:T(8,128)(2,1)S(1)}, bf16[1280,256]{1,0:T(8,128)(2,1)S(1)}, u32[]{:S(2)}, u32[]{:S(2)}) collective-permute-start(bf16[1280,256]{1,0:T(8,128)(2,1)S(1)} %tower_piece.5), channel_id=1, source_target_pairs={{0,1},{1,0},{2,3},{3,2},{4,5},{5,4},{6,7},{7,6},{8,9},{9,8},{10,11... | collective-permute-start | bytes 1966088 | tf_op jit(solution)/shard_map/ppermute | solution.py:115
  250.7 31.4 %collective-permute-start.14 = (bf16[1280,256]{1,0:T(8,128)(2,1)S(1)}, bf16[1280,256]{1,0:T(8,128)(2,1)S(1)}, u32[]{:S(2)}, u32[]{:S(2)}) collective-permute-start(bf16[1280,256]{1,0:T(8,128)(2,1)S(1)} %tower_piece.4), channel_id=1, source_target_pairs={{0,2},{1,3},{2,0},{3,1},{4,6},{5,7},{6,4},{7,5},{8,10},{9,11},{10,... | collective-permute-start | bytes 1966088 | tf_op jit(solution)/shard_map/ppermute | solution.py:115
  252.5 6.3 %collective-permute-start.28 = (f32[208,128]{1,0:T(8,128)S(1)}, f32[208,128]{1,0:T(8,128)S(1)}, u32[]{:S(2)}, u32[]{:S(2)}) collective-permute-start(f32[208,128]{1,0:T(8,128)S(1)} %fusion.22), channel_id=1, source_target_pairs={{0,16},{4,20},{8,24},{12,28},{16,0},{20,4},{24,8},{28,12},{32,48},... | collective-permute-start | bytes 319496 | tf_op jit(solution)/shard_map/ppermute | solution.py:115
  258.8 4.8 %collective-permute-start.29 = (f32[208,128]{1,0:T(8,128)S(1)}, f32[208,128]{1,0:T(8,128)S(1)}, u32[]{:S(2)}, u32[]{:S(2)}) collective-permute-start(f32[208,128]{1,0:T(8,128)S(1)} %add.108), channel_id=1, source_target_pairs={{0,32},{4,36},{8,40},{12,44},{16,48},{20,52},{24,56},{28,60},{32,0... | collective-permute-start | bytes 319496 | tf_op jit(solution)/shard_map/ppermute | solution.py:115
  263.6 8.8 %collective-permute-start.30 = (f32[208,128]{1,0:T(8,128)S(1)}, f32[208,128]{1,0:T(8,128)S(1)}, u32[]{:S(2)}, u32[]{:S(2)}) collective-permute-start(f32[208,128]{1,0:T(8,128)S(1)} %add.109), channel_id=1, source_target_pairs={{0,64},{4,68},{8,72},{12,76},{16,80},{20,84},{24,88},{28,92},{32,9... | collective-permute-start | bytes 319496 | tf_op jit(solution)/shard_map/ppermute | solution.py:115
  273.1 10.3 %copy-start.13 = (bf16[48,1,128]{2,0,1:T(8,128)(2,1)S(1)}, bf16[48,1,128]{2,0,1:T(8,128)(2,1)}, u32[]{:S(2)}) copy-start(bf16[48,1,128]{2,0,1:T(8,128)(2,1)} %copy.185) | copy-start | bytes 36868
  273.1 10.3 %copy-start.18 = (s32[416]{0:T(512)S(1)}, s32[416]{0:T(512)}, u32[]{:S(2)}) copy-start(s32[416]{0:T(512)} %constant.52.clone.table_ref) | copy-start | bytes 4996
  273.1 10.3 %copy-start.20 = (s32[48]{0:T(128)S(1)}, s32[48]{0:T(128)}, u32[]{:S(2)}) copy-start(s32[48]{0:T(128)} %copy-done.19) | copy-start | bytes 580
  273.1 17.4 %collective-permute-start.31 = (f32[208,128]{1,0:T(8,128)}, f32[208,128]{1,0:T(8,128)}, u32[]{:S(2)}, u32[]{:S(2)}) collective-permute-start(f32[208,128]{1,0:T(8,128)} %add.110), channel_id=1, source_target_pairs={{0,1},{1,0},{2,3},{3,2},{4,5},{5,4},{6,7},{7,6},{8,9},{9,8},{10,11... | collective-permute-start | bytes 319496 | tf_op jit(solution)/shard_map/ppermute | solution.py:115
  286.3 4.0 %copy-start.24 = (bf16[1280,256]{1,0:T(8,128)(2,1)S(1)}, bf16[1280,256]{1,0:T(8,128)(2,1)}, u32[]{:S(2)}) copy-start(bf16[1280,256]{1,0:T(8,128)(2,1)} %multiply_convert_fusion.1) | copy-start | bytes 1966084
  290.3 7.1 %copy-start.6 = (bf16[96,32,128]{2,1,0:T(8,128)(2,1)}, bf16[96,32,128]{2,1,0:T(8,128)(2,1)S(1)}, u32[]{:S(2)}) copy-start(bf16[96,32,128]{2,1,0:T(8,128)(2,1)S(1)} %owner_step.1) | copy-start | bytes 2359300
  290.4 13.5 %collective-permute-start.16 = (bf16[160,256]{1,0:T(8,128)(2,1)S(1)}, bf16[160,256]{1,0:T(8,128)(2,1)S(1)}, u32[]{:S(2)}, u32[]{:S(2)}) collective-permute-start(bf16[160,256]{1,0:T(8,128)(2,1)S(1)} %get-tuple-element.85), channel_id=1, source_target_pairs={{0,4},{4,0},{8,12},{12,8},{16,20},{20,16},{24,28},{28,24},{32,36},... | collective-permute-start | bytes 245768 | tf_op jit(solution)/shard_map/ppermute | solution.py:115
  291.6 33.5 %collective-permute-start.32 = (f32[208,128]{1,0:T(8,128)S(1)}, f32[208,128]{1,0:T(8,128)S(1)}, u32[]{:S(2)}, u32[]{:S(2)}) collective-permute-start(f32[208,128]{1,0:T(8,128)S(1)} %add.111), channel_id=1, source_target_pairs={{0,2},{1,3},{2,0},{3,1},{4,6},{5,7},{6,4},{7,5},{8,10},{9,11},{10,... | collective-permute-start | bytes 319496 | tf_op jit(solution)/shard_map/ppermute | solution.py:115
  293.4 12.4 %collective-permute-start.17 = (bf16[160,256]{1,0:T(8,128)(2,1)S(1)}, bf16[160,256]{1,0:T(8,128)(2,1)S(1)}, u32[]{:S(2)}, u32[]{:S(2)}) collective-permute-start(bf16[160,256]{1,0:T(8,128)(2,1)S(1)} %get-tuple-element.84), channel_id=1, source_target_pairs={{0,8},{4,12},{8,0},{12,4},{16,24},{20,28},{24,16},{28,20},{32,40},... | collective-permute-start | bytes 245768 | tf_op jit(solution)/shard_map/ppermute | solution.py:115
  295.0 10.9 %collective-permute-start.18 = (bf16[160,256]{1,0:T(8,128)(2,1)S(1)}, bf16[160,256]{1,0:T(8,128)(2,1)S(1)}, u32[]{:S(2)}, u32[]{:S(2)}) collective-permute-start(bf16[160,256]{1,0:T(8,128)(2,1)S(1)} %get-tuple-element.83), channel_id=1, source_target_pairs={{0,12},{4,8},{8,4},{12,0},{16,28},{20,24},{24,20},{28,16},{32,44},... | collective-permute-start | bytes 245768 | tf_op jit(solution)/shard_map/ppermute | solution.py:115
  295.1 12.7 %collective-permute-start.19 = (bf16[160,256]{1,0:T(8,128)(2,1)S(1)}, bf16[160,256]{1,0:T(8,128)(2,1)S(1)}, u32[]{:S(2)}, u32[]{:S(2)}) collective-permute-start(bf16[160,256]{1,0:T(8,128)(2,1)S(1)} %get-tuple-element.82), channel_id=1, source_target_pairs={{0,16},{4,20},{8,24},{12,28},{16,0},{20,4},{24,8},{28,12},{32,48},... | collective-permute-start | bytes 245768 | tf_op jit(solution)/shard_map/ppermute | solution.py:115
  297.4 39.5 %all-to-all-start.3 = ((bf16[96,1,1,32,128]{4,3,2,1,0:T(8,128)(2,1)}), bf16[96,1,1,32,128]{4,3,2,1,0:T(8,128)(2,1)S(1)}, u32[]{:S(2)}, u32[]{:S(2)}) async-start(bf16[96,1,1,32,128]{4,3,2,1,0:T(8,128)(2,1)} %bitcast.145), calls=%async_computation.3 | async-start | bytes 1572864 | tf_op jit(solution)/shard_map/all_to_all | solution.py:557
  303.9 12.7 %collective-permute-start.20 = (bf16[160,256]{1,0:T(8,128)(2,1)S(1)}, bf16[160,256]{1,0:T(8,128)(2,1)S(1)}, u32[]{:S(2)}, u32[]{:S(2)}) collective-permute-start(bf16[160,256]{1,0:T(8,128)(2,1)S(1)} %get-tuple-element.81), channel_id=1, source_target_pairs={{0,20},{4,16},{8,28},{12,24},{16,4},{20,0},{24,12},{28,8},{32,52},... | collective-permute-start | bytes 245768 | tf_op jit(solution)/shard_map/ppermute | solution.py:115
  305.8 13.1 %collective-permute-start.21 = (bf16[160,256]{1,0:T(8,128)(2,1)S(1)}, bf16[160,256]{1,0:T(8,128)(2,1)S(1)}, u32[]{:S(2)}, u32[]{:S(2)}) collective-permute-start(bf16[160,256]{1,0:T(8,128)(2,1)S(1)} %get-tuple-element.80), channel_id=1, source_target_pairs={{0,24},{4,28},{8,16},{12,20},{16,8},{20,12},{24,0},{28,4},{32,56},... | collective-permute-start | bytes 245768 | tf_op jit(solution)/shard_map/ppermute | solution.py:115
  305.9 13.6 %collective-permute-start.22 = (bf16[160,256]{1,0:T(8,128)(2,1)S(1)}, bf16[160,256]{1,0:T(8,128)(2,1)S(1)}, u32[]{:S(2)}, u32[]{:S(2)}) collective-permute-start(bf16[160,256]{1,0:T(8,128)(2,1)S(1)} %get-tuple-element.79), channel_id=1, source_target_pairs={{0,28},{4,24},{8,20},{12,16},{16,12},{20,8},{24,4},{28,0},{32,60},... | collective-permute-start | bytes 245768 | tf_op jit(solution)/shard_map/ppermute | solution.py:115
  321.2 6.8 %collective-permute-start.23 = (bf16[282,256]{1,0:T(8,128)(2,1)S(1)}, bf16[282,256]{1,0:T(8,128)(2,1)S(1)}, u32[]{:S(2)}, u32[]{:S(2)}) collective-permute-start(bf16[282,256]{1,0:T(8,128)(2,1)S(1)} %get-tuple-element.96), channel_id=1, source_target_pairs={{0,1},{1,0},{2,3},{3,2},{4,5},{5,4},{6,7},{7,6},{8,9},{9,8},{10,11... | collective-permute-start | bytes 433160 | tf_op jit(solution)/shard_map/ppermute | solution.py:115
  322.5 10.0 %collective-permute-start.24 = (bf16[282,256]{1,0:T(8,128)(2,1)S(1)}, bf16[282,256]{1,0:T(8,128)(2,1)S(1)}, u32[]{:S(2)}, u32[]{:S(2)}) collective-permute-start(bf16[282,256]{1,0:T(8,128)(2,1)S(1)} %get-tuple-element.95), channel_id=1, source_target_pairs={{0,2},{1,3},{2,0},{3,1},{4,6},{5,7},{6,4},{7,5},{8,10},{9,11},{10,... | collective-permute-start | bytes 433160 | tf_op jit(solution)/shard_map/ppermute | solution.py:115
  325.1 8.7 %collective-permute-start.25 = (bf16[282,256]{1,0:T(8,128)(2,1)S(1)}, bf16[282,256]{1,0:T(8,128)(2,1)S(1)}, u32[]{:S(2)}, u32[]{:S(2)}) collective-permute-start(bf16[282,256]{1,0:T(8,128)(2,1)S(1)} %get-tuple-element.97), channel_id=1, source_target_pairs={{0,3},{1,2},{2,1},{3,0},{4,7},{5,6},{6,5},{7,4},{8,11},{9,10},{10,... | collective-permute-start | bytes 433160 | tf_op jit(solution)/shard_map/ppermute | solution.py:115
  335.7 2.2 copy-start.1
  (8 other events, 7.3 us)
Sparse Core Ops, SparseCore 0:
  10.2 111.1 all-gather.1

commit v2 on v1

--- a/solution.py
+++ b/solution.py
@@ -119,9 +119,18 @@
     return [blocks[0]] + [swap(b, axis, size, k) for k, b in enumerate(blocks) if k]
 
 
+def sum_of_four(value, axis, size, step):
+    one, two, three = [swap(value, axis, size, k * step) for k in (1, 2, 3)]
+    return (value + one) + (two + three)
+
+
 def xor_order(blocks, axis):
     own = lax.axis_index(axis)
     return jnp.take(blocks, own ^ jnp.arange(blocks.shape[0], dtype=jnp.int32), axis=0, mode="clip")
+
+
+def off_chip(x):
+    return pltpu.with_memory_space_constraint(x, pltpu.HBM)
 
 
 def halves(x):
@@ -201,15 +210,17 @@
             flops=2 * tall * hidden * cols, transcendentals=0, bytes_accessed=30_000_000
         ),
         name="tower_pairs",
-    )(own, *pieces, cotangent)
-
-
-def tower_piece(own, pairs, cotangent, parts, k):
+    )(own, *[off_chip(p) for p in pieces], off_chip(cotangent))
+
+
+def tower_total(own, pairs, cotangent, parts):
     tall, cols = pairs.shape
-    quarter = cotangent.shape[0] // parts
+    hidden = cotangent.shape[0]
+    quarter = hidden // parts
     step = 512
 
-    def body(own_ref, pairs_ref, cot_ref, out_ref, acc):
+    def body(own_ref, pairs_ref, cot_ref, *refs):
+        outs, acc = refs[:parts], refs[parts]
         i = pl.program_id(0)
 
         @pl.when(i == 0)
@@ -225,27 +236,35 @@
 
         @pl.when(i == pl.num_programs(0) - 1)
         def _():
-            out_ref[...] = acc[...].astype(out_ref.dtype)
+            for o in range(parts):
+
+                @pl.when(own_ref[0] == o)
+                def _(o=o):
+                    for k in range(parts):
+                        q = o ^ k
+                        outs[k][...] = acc[:, q * quarter : (q + 1) * quarter].astype(
+                            pairs.dtype
+                        )
 
     return pl.pallas_call(
         body,
-        out_shape=jax.ShapeDtypeStruct((tall, quarter), pairs.dtype),
+        out_shape=[jax.ShapeDtypeStruct((tall, quarter), pairs.dtype)] * parts,
         grid_spec=pltpu.PrefetchScalarGridSpec(
             num_scalar_prefetch=1,
             grid=(cols // step,),
             in_specs=[
-                pl.BlockSpec((tall, step), lambda i, own_ref: (0, i)),
-                pl.BlockSpec((quarter, step), lambda i, own_ref: (own_ref[0] ^ k, i)),
-            ],
-            out_specs=pl.BlockSpec((tall, quarter), lambda i, own_ref: (0, 0)),
-            scratch_shapes=[pltpu.VMEM((tall, quarter), jnp.float32)],
-        ),
-        compiler_params=pltpu.CompilerParams(vmem_limit_bytes=16 * 1024 * 1024),
+                pl.BlockSpec((tall, step), lambda i, *_: (0, i)),
+                pl.BlockSpec((hidden, step), lambda i, *_: (0, i)),
+            ],
+            out_specs=[pl.BlockSpec((tall, quarter), lambda i, *_: (0, 0))] * parts,
+            scratch_shapes=[pltpu.VMEM((tall, hidden), jnp.float32)],
+        ),
+        compiler_params=pltpu.CompilerParams(vmem_limit_bytes=32 * 1024 * 1024),
         cost_estimate=pl.CostEstimate(
-            flops=2 * tall * quarter * cols, transcendentals=0, bytes_accessed=14_000_000
-        ),
-        name="tower_piece",
-    )(own, pairs, cotangent)
+            flops=2 * tall * hidden * cols, transcendentals=0, bytes_accessed=20_000_000
+        ),
+        name="tower_total",
+    )(own, off_chip(pairs), off_chip(cotangent))
 
 
 def owner_step(parts, selected, squeezed, table, slot_index, w_ex, w_ext, w_sq, w_sqt, slots):
@@ -318,7 +337,7 @@
         ),
         compiler_params=pltpu.CompilerParams(vmem_limit_bytes=40 * 1024 * 1024),
         name="owner_step",
-    )(table, slot_index, parts, *mats)
+    )(table, slot_index, off_chip(parts), *mats)
 
 
 def pair_step(got, pair_grad, left, right, signs, w_pairs, w_ex, w_ext, w_sq, width):
@@ -455,7 +474,7 @@
         ),
         compiler_params=pltpu.CompilerParams(vmem_limit_bytes=40 * 1024 * 1024),
         name="pair_step",
-    )(left, right, got, pair_grad, *mats)
+    )(left, right, off_chip(got), pair_grad, *mats)
 
 
 def on_device(pooled, field_owner, w_squeeze, w_excite, w_bilinear, tower_weight, tower_cotangent):
@@ -495,7 +514,6 @@
     cut = cut.reshape(plane, depth * width, quarter)
 
     sent = pack_rows(received, squeeze_rows, slot_index, table)
-    sent, cut = lax.optimization_barrier((sent, cut))
     got = lax.all_to_all(sent, "table", split_axis=0, concat_axis=0, tiled=True)
     cut = trade([cut[k] for k in range(plane)], "table", tables)
     cut = jnp.concatenate(cut, axis=0)
@@ -528,15 +546,11 @@
     )
     parts = lax.all_to_all(part, "table", split_axis=0, concat_axis=0, tiled=True)
 
-    own_now = own_sub[None]
-    total = [None] * subs
-    for k in sorted(range(subs), key=lambda k: (k == 0, k != 2, k)):
-        piece = tower_piece(own_now, pairs, cotangent, subs, k)
-        own_now, piece = lax.optimization_barrier((own_now, piece))
-        total[k] = swap(piece, "sub", subs, k) if k else piece
-    d_excite, d_squeeze, d_bilinear, _ = lax.optimization_barrier(
-        (d_excite, d_squeeze, d_bilinear, own_now)
-    )
+    total = tower_total(own_sub[None], pairs, cotangent, subs)
+    sent = [total[0]]
+    for k in range(1, subs):
+        sent.append(swap(total[k], "sub", subs, k))
+    total = sent
     total = sum(x.astype(f32) for x in total) * (1.0 / total_samples)
     bundled = [x.T.reshape(w_squeeze.shape[0], count // 8, 8 * width).transpose(1, 0, 2) for x in (xh, xl)]
     placed = owner_step(
@@ -552,7 +566,6 @@
         per_owner * tables,
     )
     total = total.astype(bf16)
-    placed, total = lax.optimization_barrier((placed, total))
     placed = placed.reshape(per_owner * tables, 1, 1, width, samples)
     row_grads = lax.all_to_all(placed, "table", split_axis=0, concat_axis=1, tiled=True)
     total = total.reshape(plane, depth * width, quarter)
@@ -582,11 +595,10 @@
     small = jnp.concatenate([d_excite.reshape(-1), d_squeeze.reshape(-1), d_bilinear.reshape(-1)])
     ends = np.cumsum([w_excite.size, w_squeeze.size, w_bilinear.size])
     small = jnp.pad(small, (0, -small.size % 1024)).reshape(-1, 128)
-    for axis, size in (("table", tables), ("sub", subs)):
-        bit = 1
-        while bit < size:
-            small = small + swap(small, axis, size, bit)
-            bit *= 2
+    small = small + swap(small, "table", tables, 1)
+    small = sum_of_four(small, "sub", subs, 1)
+    for bit in range(1, tables.bit_length() - 1, 2):
+        small = sum_of_four(small, "table", tables, 2**bit)
     small = small.reshape(-1) * (1.0 / total_samples)
     g_excite = small[: ends[0]].reshape(w_excite.shape)
     g_squeeze = small[ends[0] : ends[1]].reshape(w_squeeze.shape)

time: 350 us -> 336 us (0.960)
  local copies, waits for them, and re-layouts: 46.9 us -> 23.7 us
  waiting for transfers between devices: 126 us -> 147 us
  other arithmetic: 9.11 us -> 2.25 us
    ppermute x33 -> x36, waiting for transfers between devices: 116 us -> 132 us  [swap(): return lax.ppermute(value, axis, [(a, a ^ k) for a in range(size)])]
    unnamed x88 -> x62, local copies, waits for them, and re-layouts: 23.1 us -> 7.62 us
    pallas_call x4 -> x1, Pallas kernels: 22.1 us -> 15.1 us  [tower_total(): pl.pallas_call(body, out_shape=[jax.ShapeDtypeStruct((tall, quarter), pai...]
    ppermute x33 -> x36, starting transfers between devices: 46.2 us -> 43.9 us  [swap(): return lax.ppermute(value, axis, [(a, a ^ k) for a in range(size)])]
  transfers between devices with their start and end apart: 38 -> 41, of which waited for: 17 -> 21; matrix products, arithmetic and copies ran while one was open for 11% -> 6% of each run, Pallas kernels for 13% -> 13%
where the time goes in v2:
time: 336 us; the launch traced here: 332 us
  waiting for transfers between devices  147 us (44%)
  starting transfers between devices  74.5 us (22%)
  Pallas kernels  68.7 us (20%)
  local copies, waits for them, and re-layouts  23.7 us (7%)
  between operations  14.8 us (4%)
    ppermute x36, waiting for transfers between devices, swap(): return lax.ppermute(value, axis, [(a, a ^ k) for a in range(size)])  132 us
    ppermute x36, starting transfers between devices, swap(): return lax.ppermute(value, axis, [(a, a ^ k) for a in range(size)])  43.9 us
    pallas_call x1, Pallas kernels, pair_step(): pl.pallas_call(body, out_shape=(jax.ShapeDtypeStruct((slots * width, tabl...  26.2 us
    pallas_call x1, Pallas kernels, tower_pairs(): pl.pallas_call(body, out_shape=jax.ShapeDtypeStruct((tall, cols), cotange...  15.6 us
    pallas_call x1, Pallas kernels, tower_total(): pl.pallas_call(body, out_shape=[jax.ShapeDtypeStruct((tall, quarter), pai...  15.1 us
    all_to_all x1, waiting for transfers between devices, on_device(): lax.all_to_all(rotated, 'table', split_axis=1, concat_axis=0, tiled=True)  13.6 us
    all_to_all x1, starting transfers between devices, on_device(): lax.all_to_all(rotated, 'table', split_axis=1, concat_axis=0, tiled=True)  8.59 us
    all_to_all x1, starting transfers between devices, on_device(): lax.all_to_all(placed, 'table', split_axis=0, concat_axis=1, tiled=True)  8.54 us
  transfers between devices with their start and end apart: 41, of which 21 were waited for; matrix products, arithmetic and copies ran while one was open for 6% of the time, Pallas kernels for 13%

profile of v2, /device:TPU:10, one launch (start us, length us, event | category | flops | bytes accessed | tf_op | source)
XLA Modules:
  0.0 331.8 jit_solution(7811378168927547676)
XLA Ops:
  7.2 0.7 all-gather.2.cloned.1.call-update
  8.3 1.0 fusion
  10.9 2.6 collective-permute-start.1
  14.0 0.9 copy.149
  14.9 8.6 %all-to-all-start = ((bf16[3,32,1,32,128]{4,3,0,2,1:T(8,128)(2,1)}), bf16[3,32,1,32,128]{4,3,0,2,1:T(8,128)(2,1)S(1)}, u32[]{:S(2)}, u32[]{:S(2)}) async-start(bf16[3,32,1,32,128]{4,3,0,2,1:T(8,128)(2,1)} %copy.149), calls=%async_computation | async-start | bytes 1572864 | tf_op jit(solution)/shard_map/all_to_all | solution.py:499
  24.0 0.7 fusion.16
  24.7 0.7 constant_dynamic-slice_fusion.2
  25.7 13.6 %all-to-all-done = bf16[3,32,1,32,128]{4,3,0,2,1:T(8,128)(2,1)S(1)} async-done(((bf16[3,32,1,32,128]{4,3,0,2,1:T(8,128)(2,1)}), bf16[3,32,1,32,128]{4,3,0,2,1:T(8,128)(2,1)S(1)}, u32[]{:S(2)}, u32[]{:S(2)}) %all-to-all-start) | async-done | bytes 786464 | tf_op jit(solution)/shard_map/all_to_all | solution.py:499
  40.7 4.4 %pack_rows.1 = bf16[32,464,128]{2,1,0:T(8,128)(2,1)} custom-call(s32[48]{0:T(128)} %copy-done.10, s32[416]{0:T(512)} %constant.52.clone.table_ref, bf16[96,32,128]{2,1,0:T(8,128)(2,1)} %bitcast.150, bf16[48,128]{1,0:T(8,128)(2,1)} %bitcast.147), custom_call_target="tpu_custom_call" | custom-call | tf_op jit(solution)/shard_map/pack_rows/pallas_call | solution.py:157
  45.1 6.4 %all-to-all-start.1 = ((bf16[32,464,128]{2,1,0:T(8,128)(2,1)}), bf16[32,464,128]{2,1,0:T(8,128)(2,1)}, u32[]{:S(2)}, u32[]{:S(2)}) async-start(bf16[32,464,128]{2,1,0:T(8,128)(2,1)} %pack_rows.1), calls=%async_computation.1 | async-start | bytes 7602176 | tf_op jit(solution)/shard_map/all_to_all | solution.py:517
  51.4 0.7 fusion.14
  54.1 0.7 dynamic-slice_bitcast_fusion
  56.2 0.7 gather_fusion.3
  57.6 1.3 collective-permute-start.5
  59.0 2.1 collective-permute-start.6
  61.0 1.2 collective-permute-start.7
  62.2 1.5 collective-permute-start.8
  63.7 42.2 %collective-permute-done.4 = bf16[160,256]{1,0:T(8,128)(2,1)S(1)} collective-permute-done((bf16[160,256]{1,0:T(8,128)(2,1)S(1)}, bf16[160,256]{1,0:T(8,128)(2,1)S(1)}, u32[]{:S(2)}, u32[]{:S(2)}) %collective-permute-start.4) | collective-permute-done | bytes 81952 | tf_op jit(solution)/shard_map/ppermute | solution.py:115
  105.9 2.2 collective-permute-start.9
  108.6 6.6 %collective-permute-done.6 = bf16[160,256]{1,0:T(8,128)(2,1)S(1)} collective-permute-done((bf16[160,256]{1,0:T(8,128)(2,1)S(1)}, bf16[160,256]{1,0:T(8,128)(2,1)S(1)}, u32[]{:S(2)}, u32[]{:S(2)}) %collective-permute-start.6) | collective-permute-done | bytes 81952 | tf_op jit(solution)/shard_map/ppermute | solution.py:115
  115.2 2.6 collective-permute-done.7
  117.9 1.0 collective-permute-start.10
  119.0 2.0 collective-permute-start.11
  121.6 14.0 %collective-permute-done.10.refs_1_ = bf16[1280,256]{1,0:T(8,128)(2,1)S(1)} collective-permute-done((bf16[1280,256]{1,0:T(8,128)(2,1)S(1)}, bf16[1280,256]{1,0:T(8,128)(2,1)S(1)}, u32[]{:S(2)}, u32[]{:S(2)}) %collective-permute-start.10) | collective-permute-done | bytes 655392 | tf_op jit(solution)/shard_map/ppermute | solution.py:115
  135.6 14.5 %collective-permute-done.11.refs_2_ = bf16[1280,256]{1,0:T(8,128)(2,1)S(1)} collective-permute-done((bf16[1280,256]{1,0:T(8,128)(2,1)S(1)}, bf16[1280,256]{1,0:T(8,128)(2,1)S(1)}, u32[]{:S(2)}, u32[]{:S(2)}) %collective-permute-start.11) | collective-permute-done | bytes 655392 | tf_op jit(solution)/shard_map/ppermute | solution.py:115
  150.2 1.5 collective-permute-done.12.refs_3_
  151.7 15.6 %tower_pairs.1.pg_ref = bf16[1280,4096]{1,0:T(8,128)(2,1)S(1)} custom-call(s32[1]{0:T(128)} %bitcast.14.own_ref, bf16[1280,256]{1,0:T(8,128)(2,1)} %copy-done.17, bf16[1280,256]{1,0:T(8,128)(2,1)} %copy-done.18, bf16[1280,256]{1,0:T(8,128)(2,1)} %copy-done.19, bf16[1280,256]{1,0:T(8,128)(2,1)} %collective-permute-done.12.refs_3_, ...), custom_call_target="tpu_custom_call" | custom-call | flops 10737418240 | bytes 30000000 | tf_op jit(solution)/shard_map/tower_pairs/pallas_call | solution.py:195
  167.3 3.9 %copy-done.2 = bf16[1280,4096]{1,0:T(8,128)(2,1)} copy-done((bf16[1280,4096]{1,0:T(8,128)(2,1)}, bf16[1280,4096]{1,0:T(8,128)(2,1)S(1)}, u32[]{:S(2)}) %copy-start.2) | copy-done | bytes 10485784
  171.2 26.2 %pair_step.1 = (bf16[1280,4096]{1,0:T(8,128)(2,1)}, bf16[32,416,128]{2,1,0:T(8,128)(2,1)}, f32[416,224]{1,0:T(8,128)S(1)}, f32[32,416]{1,0:T(8,128)S(1)}, f32[32,48]{1,0:T(8,128)S(1)}) custom-call(s32[40]{0:T(128)S(1)} %get-tuple-element.86.left_ref, s32[40]{0:T(128)S(1)} %get-tuple-element.87.right_ref, bf16[32,464,128]{2,1,0:T(8,128)(2,1)} %all-to-all-done.1.got_ref, ...), custom_call_target="tpu_custom_call" | custom-call | tf_op jit(solution)/shard_map/pair_step/pallas_call | solution.py:446
  198.4 7.0 %all-to-all-start.2 = ((bf16[32,416,128]{2,1,0:T(8,128)(2,1)}), bf16[32,416,128]{2,1,0:T(8,128)(2,1)}, u32[]{:S(2)}, u32[]{:S(2)}) async-start(bf16[32,416,128]{2,1,0:T(8,128)(2,1)} %get-tuple-element.18), calls=%async_computation.2 | async-start | bytes 6815744 | tf_op jit(solution)/shard_map/all_to_all | solution.py:547
  205.4 15.1 %tower_total.1 = (bf16[1280,256]{1,0:T(8,128)(2,1)S(1)}, bf16[1280,256]{1,0:T(8,128)(2,1)S(1)}, bf16[1280,256]{1,0:T(8,128)(2,1)S(1)}, bf16[1280,256]{1,0:T(8,128)(2,1)S(1)}) custom-call(s32[1]{0:T(128)} %bitcast.14.own_ref, bf16[1280,4096]{1,0:T(8,128)(2,1)} %get-tuple-element.19.pairs_ref, bf16[1024,4096]{1,0:T(8,128)(2,1)} %all-gather.2.cloned.1.call-done.refs_4_.cot_ref), custom_call_target="tpu_custom_call" | custom-call | flops 10737418240 | bytes 20000000 | tf_op jit(solution)/shard_map/tower_total/pallas_call | solution.py:249
  220.5 3.6 %collective-permute-start.13 = (bf16[1280,256]{1,0:T(8,128)(2,1)S(1)}, bf16[1280,256]{1,0:T(8,128)(2,1)S(1)}, u32[]{:S(2)}, u32[]{:S(2)}) collective-permute-start(bf16[1280,256]{1,0:T(8,128)(2,1)S(1)} %get-tuple-element.21), channel_id=1, source_target_pairs={{0,1},{1,0},{2,3},{3,2},{4,5},{5,4},{6,7},{7,6},{8,9},{9,8},{10,11... | collective-permute-start | bytes 1966088 | tf_op jit(solution)/shard_map/ppermute | solution.py:115
  224.1 1.6 collective-permute-start.15
  225.7 3.2 collective-permute-start.27
  228.9 0.7 constant_dynamic-slice_fusion
  229.6 26.4 %collective-permute-done.27 = f32[208,128]{1,0:T(8,128)S(1)} collective-permute-done((f32[208,128]{1,0:T(8,128)S(1)}, f32[208,128]{1,0:T(8,128)S(1)}, u32[]{:S(2)}, u32[]{:S(2)}) %collective-permute-start.27) | collective-permute-done | bytes 106528 | tf_op jit(solution)/shard_map/ppermute | solution.py:115
  256.1 1.0 collective-permute-done.28
  257.0 3.7 %collective-permute-done.29 = f32[208,128]{1,0:T(8,128)S(1)} collective-permute-done((f32[208,128]{1,0:T(8,128)S(1)}, f32[208,128]{1,0:T(8,128)S(1)}, u32[]{:S(2)}, u32[]{:S(2)}) %collective-permute-start.29) | collective-permute-done | bytes 106528 | tf_op jit(solution)/shard_map/ppermute | solution.py:115
  261.2 2.6 collective-permute-start.31
  264.9 1.2 collective-permute-done.30
  266.1 1.5 collective-permute-done.31
  267.6 1.1 collective-permute-done.32
  268.8 1.6 collective-permute-start.33
  270.4 2.7 collective-permute-start.34
  273.6 2.7 collective-permute-start.17
  276.3 2.5 collective-permute-done.17
  278.8 2.4 collective-permute-start.19
  281.6 3.2 collective-permute-done.19
  285.4 1.3 collective-permute-done.20
  286.7 2.5 collective-permute-done.21
  289.2 2.1 collective-permute-done.22
  291.3 0.7 gather_fusion.6
  293.0 7.3 %owner_step.1 = bf16[96,32,128]{2,1,0:T(8,128)(2,1)} custom-call(s32[416]{0:T(512)S(1)} %copy-done.9, s32[48]{0:T(128)S(1)} %copy-done.11, bf16[32,416,128]{2,1,0:T(8,128)(2,1)} %all-to-all-done.2.parts_ref, bf16[48,32,128]{2,1,0:T(8,128)(2,1)S(1)} %gather_fusion, bf16[48,128]{1,0:T(8,128)(2,1)S(1)} %bitcast.148, bf16[256,256]{1,0:T(8,128)(2,1)S(1)} %copy-done.5, ...), custom_call_target="tpu_custom_call" | custom-call | tf_op jit(solution)/shard_map/owner_step/pallas_call | solution.py:321
  300.3 8.5 %all-to-all-start.3 = ((bf16[96,1,1,32,128]{4,3,2,1,0:T(8,128)(2,1)}), bf16[96,1,1,32,128]{4,3,2,1,0:T(8,128)(2,1)S(1)}, u32[]{:S(2)}, u32[]{:S(2)}) async-start(bf16[96,1,1,32,128]{4,3,2,1,0:T(8,128)(2,1)} %bitcast.47), calls=%async_computation.3 | async-start | bytes 1572864 | tf_op jit(solution)/shard_map/all_to_all | solution.py:570
  308.9 3.3 collective-permute-start.23
  312.3 1.5 collective-permute-start.25
  313.8 0.9 add_multiply_fusion
  315.0 0.9 copy.171
  315.9 0.7 slice.206
  317.2 2.3 collective-permute-done.24
  319.6 1.5 collective-permute-done.25
  321.8 0.7 copy.169
  322.8 1.2 copy.176
  324.0 0.9 copy.183
  (174 shorter events, 16.3 us)
Async XLA Ops:
  7.2 1.1 copy-start
  7.2 2.2 copy-start.13
  7.2 144.4 %all-gather.2.cloned.1.call-start = ((), (), s32[]{:S(2)}) async-start(), calls=%async_computation.4 | async-start | bytes 8650752 | tf_op jit(solution)/shard_map/all_gather | solution.py:522
  10.4 44.9 %collective-permute-start = (bf16[282,256]{1,0:T(8,128)(2,1)S(1)}, bf16[282,256]{1,0:T(8,128)(2,1)S(1)}, u32[]{:S(2)}, u32[]{:S(2)}) collective-permute-start(bf16[282,256]{1,0:T(8,128)(2,1)S(1)} %get-tuple-element.80), channel_id=1, source_target_pairs={{0,1},{1,0},{2,3},{3,2},{4,5},{5,4},{6,7},{7,6},{8,9},{9,8},{10,11... | collective-permute-start | bytes 433160 | tf_op jit(solution)/shard_map/ppermute | solution.py:115
  10.9 44.4 %collective-permute-start.1 = (bf16[282,256]{1,0:T(8,128)(2,1)S(1)}, bf16[282,256]{1,0:T(8,128)(2,1)S(1)}, u32[]{:S(2)}, u32[]{:S(2)}) collective-permute-start(bf16[282,256]{1,0:T(8,128)(2,1)S(1)} %get-tuple-element.79), channel_id=1, source_target_pairs={{0,2},{1,3},{2,0},{3,1},{4,6},{5,7},{6,4},{7,5},{8,10},{9,11},{10,... | collective-permute-start | bytes 433160 | tf_op jit(solution)/shard_map/ppermute | solution.py:115
  13.5 10.0 %copy-start.16 = (f32[16,48]{1,0:T(8,128)S(1)}, f32[16,48]{1,0:T(8,128)}, u32[]{:S(2)}) copy-start(f32[16,48]{1,0:T(8,128)} %param.22) | copy-start | bytes 9220
  13.5 10.4 %copy-start.15 = (f32[32,32]{1,0:T(8,128)S(1)}, f32[32,32]{1,0:T(8,128)}, u32[]{:S(2)}) copy-start(f32[32,32]{1,0:T(8,128)} %param.24) | copy-start | bytes 12292
  13.5 11.9 %copy-start.20 = (s32[48]{0:T(128)S(1)}, s32[48]{0:T(128)}, u32[]{:S(2)}) copy-start(s32[48]{0:T(128)} %param.21) | copy-start | bytes 580
  13.5 41.8 %collective-permute-start.2 = (bf16[282,256]{1,0:T(8,128)(2,1)S(1)}, bf16[282,256]{1,0:T(8,128)(2,1)S(1)}, u32[]{:S(2)}, u32[]{:S(2)}) collective-permute-start(bf16[282,256]{1,0:T(8,128)(2,1)S(1)} %get-tuple-element.81), channel_id=1, source_target_pairs={{0,3},{1,2},{2,1},{3,0},{4,7},{5,6},{6,5},{7,4},{8,11},{9,10},{10,... | collective-permute-start | bytes 433160 | tf_op jit(solution)/shard_map/ppermute | solution.py:115
  14.9 10.8 %copy-start.14 = (f32[1536,16]{0,1:T(8,128)S(1)}, f32[1536,16]{0,1:T(8,128)}, u32[]{:S(2)}) copy-start(f32[1536,16]{0,1:T(8,128)} %param.23) | copy-start | bytes 294916
  14.9 24.5 %all-to-all-start = ((bf16[3,32,1,32,128]{4,3,0,2,1:T(8,128)(2,1)}), bf16[3,32,1,32,128]{4,3,0,2,1:T(8,128)(2,1)S(1)}, u32[]{:S(2)}, u32[]{:S(2)}) async-start(bf16[3,32,1,32,128]{4,3,0,2,1:T(8,128)(2,1)} %copy.149), calls=%async_computation | async-start | bytes 1572864 | tf_op jit(solution)/shard_map/all_to_all | solution.py:499
  25.7 15.0 %copy-start.10 = (s32[48]{0:T(128)}, s32[48]{0:T(128)S(1)}, u32[]{:S(2)}) copy-start(s32[48]{0:T(128)S(1)} %multiply_add_fusion.slot_ref) | copy-start | bytes 580
  39.4 1.3 copy-start.12
  45.1 126.1 %all-to-all-start.1 = ((bf16[32,464,128]{2,1,0:T(8,128)(2,1)}), bf16[32,464,128]{2,1,0:T(8,128)(2,1)}, u32[]{:S(2)}, u32[]{:S(2)}) async-start(bf16[32,464,128]{2,1,0:T(8,128)(2,1)} %pack_rows.1), calls=%async_computation.1 | async-start | bytes 7602176 | tf_op jit(solution)/shard_map/all_to_all | solution.py:517
  57.0 5.2 %collective-permute-start.3 = (bf16[160,256]{1,0:T(8,128)(2,1)S(1)}, bf16[160,256]{1,0:T(8,128)(2,1)S(1)}, u32[]{:S(2)}, u32[]{:S(2)}) collective-permute-start(bf16[160,256]{1,0:T(8,128)(2,1)S(1)} %get-tuple-element.73), channel_id=1, source_target_pairs={{0,4},{4,0},{8,12},{12,8},{16,20},{20,16},{24,28},{28,24},{32,36},... | collective-permute-start | bytes 245768 | tf_op jit(solution)/shard_map/ppermute | solution.py:115
  57.2 48.7 %collective-permute-start.4 = (bf16[160,256]{1,0:T(8,128)(2,1)S(1)}, bf16[160,256]{1,0:T(8,128)(2,1)S(1)}, u32[]{:S(2)}, u32[]{:S(2)}) collective-permute-start(bf16[160,256]{1,0:T(8,128)(2,1)S(1)} %get-tuple-element.72), channel_id=1, source_target_pairs={{0,8},{4,12},{8,0},{12,4},{16,24},{20,28},{24,16},{28,20},{32,40},... | collective-permute-start | bytes 245768 | tf_op jit(solution)/shard_map/ppermute | solution.py:115
  57.6 50.9 %collective-permute-start.5 = (bf16[160,256]{1,0:T(8,128)(2,1)S(1)}, bf16[160,256]{1,0:T(8,128)(2,1)S(1)}, u32[]{:S(2)}, u32[]{:S(2)}) collective-permute-start(bf16[160,256]{1,0:T(8,128)(2,1)S(1)} %get-tuple-element.71), channel_id=1, source_target_pairs={{0,12},{4,8},{8,4},{12,0},{16,28},{20,24},{24,20},{28,16},{32,44},... | collective-permute-start | bytes 245768 | tf_op jit(solution)/shard_map/ppermute | solution.py:115
  59.0 56.3 %collective-permute-start.6 = (bf16[160,256]{1,0:T(8,128)(2,1)S(1)}, bf16[160,256]{1,0:T(8,128)(2,1)S(1)}, u32[]{:S(2)}, u32[]{:S(2)}) collective-permute-start(bf16[160,256]{1,0:T(8,128)(2,1)S(1)} %get-tuple-element.70), channel_id=1, source_target_pairs={{0,16},{4,20},{8,24},{12,28},{16,0},{20,4},{24,8},{28,12},{32,48},... | collective-permute-start | bytes 245768 | tf_op jit(solution)/shard_map/ppermute | solution.py:115
  61.0 56.8 %collective-permute-start.7 = (bf16[160,256]{1,0:T(8,128)(2,1)S(1)}, bf16[160,256]{1,0:T(8,128)(2,1)S(1)}, u32[]{:S(2)}, u32[]{:S(2)}) collective-permute-start(bf16[160,256]{1,0:T(8,128)(2,1)S(1)} %get-tuple-element.69), channel_id=1, source_target_pairs={{0,20},{4,16},{8,28},{12,24},{16,4},{20,0},{24,12},{28,8},{32,52},... | collective-permute-start | bytes 245768 | tf_op jit(solution)/shard_map/ppermute | solution.py:115
  62.2 55.6 %collective-permute-start.8 = (bf16[160,256]{1,0:T(8,128)(2,1)S(1)}, bf16[160,256]{1,0:T(8,128)(2,1)S(1)}, u32[]{:S(2)}, u32[]{:S(2)}) collective-permute-start(bf16[160,256]{1,0:T(8,128)(2,1)S(1)} %get-tuple-element.68), channel_id=1, source_target_pairs={{0,24},{4,28},{8,16},{12,20},{16,8},{20,12},{24,0},{28,4},{32,56},... | collective-permute-start | bytes 245768 | tf_op jit(solution)/shard_map/ppermute | solution.py:115
  105.9 11.9 %collective-permute-start.9 = (bf16[160,256]{1,0:T(8,128)(2,1)S(1)}, bf16[160,256]{1,0:T(8,128)(2,1)S(1)}, u32[]{:S(2)}, u32[]{:S(2)}) collective-permute-start(bf16[160,256]{1,0:T(8,128)(2,1)S(1)} %get-tuple-element.67), channel_id=1, source_target_pairs={{0,28},{4,24},{8,20},{12,16},{16,12},{20,8},{24,4},{28,0},{32,60},... | collective-permute-start | bytes 245768 | tf_op jit(solution)/shard_map/ppermute | solution.py:115
  117.9 3.6 %copy-start.17 = (bf16[1280,256]{1,0:T(8,128)(2,1)}, bf16[1280,256]{1,0:T(8,128)(2,1)S(1)}, u32[]{:S(2)}) copy-start(bf16[1280,256]{1,0:T(8,128)(2,1)S(1)} %constant_dynamic-update-slice_fusion.refs_0_) | copy-start | bytes 1966084
  117.9 17.7 %collective-permute-start.10 = (bf16[1280,256]{1,0:T(8,128)(2,1)S(1)}, bf16[1280,256]{1,0:T(8,128)(2,1)S(1)}, u32[]{:S(2)}, u32[]{:S(2)}) collective-permute-start(bf16[1280,256]{1,0:T(8,128)(2,1)S(1)} %constant_dynamic-update-slice_fusion.refs_0_), channel_id=1, source_target_pairs={{0,1},{1,0},{2,3},{3,2},{4,5},{5,4},{6,7},{7,6},{8,9},{9,8},{10,11... | collective-permute-start | bytes 1966088 | tf_op jit(solution)/shard_map/ppermute | solution.py:115
  119.0 31.2 %collective-permute-start.11 = (bf16[1280,256]{1,0:T(8,128)(2,1)S(1)}, bf16[1280,256]{1,0:T(8,128)(2,1)S(1)}, u32[]{:S(2)}, u32[]{:S(2)}) collective-permute-start(bf16[1280,256]{1,0:T(8,128)(2,1)S(1)} %constant_dynamic-update-slice_fusion.refs_0_), channel_id=1, source_target_pairs={{0,2},{1,3},{2,0},{3,1},{4,6},{5,7},{6,4},{7,5},{8,10},{9,11},{10,... | collective-permute-start | bytes 1966088 | tf_op jit(solution)/shard_map/ppermute | solution.py:115
  120.9 30.7 %collective-permute-start.12 = (bf16[1280,256]{1,0:T(8,128)(2,1)S(1)}, bf16[1280,256]{1,0:T(8,128)(2,1)}, u32[]{:S(2)}, u32[]{:S(2)}) collective-permute-start(bf16[1280,256]{1,0:T(8,128)(2,1)S(1)} %constant_dynamic-update-slice_fusion.refs_0_), channel_id=1, source_target_pairs={{0,3},{1,2},{2,1},{3,0},{4,7},{5,6},{6,5},{7,4},{8,11},{9,10},{10,... | collective-permute-start | bytes 1966088 | tf_op jit(solution)/shard_map/ppermute | solution.py:115
  135.6 16.0 %copy-start.18 = (bf16[1280,256]{1,0:T(8,128)(2,1)}, bf16[1280,256]{1,0:T(8,128)(2,1)S(1)}, u32[]{:S(2)}) copy-start(bf16[1280,256]{1,0:T(8,128)(2,1)S(1)} %collective-permute-done.10.refs_1_) | copy-start | bytes 1966084
  150.2 1.5 copy-start.19
  151.6 19.5 %copy-start.3 = (f32[416,224]{1,0:T(8,128)S(1)}, f32[416,224]{1,0:T(8,128)}, u32[]{:S(2)}) copy-start(f32[416,224]{1,0:T(8,128)} %constant.60.clone.mask_ref) | copy-start | bytes 1118212
  151.6 19.5 %copy-start.4 = (bf16[416,224]{1,0:T(8,128)(2,1)S(1)}, bf16[416,224]{1,0:T(8,128)(2,1)}, u32[]{:S(2)}) copy-start(bf16[416,224]{1,0:T(8,128)(2,1)} %constant.57.clone.hd_ref) | copy-start | bytes 559108
  151.7 19.5 %copy-start.7 = (bf16[416,32]{1,0:T(8,128)(2,1)S(1)}, bf16[416,32]{1,0:T(8,128)(2,1)}, u32[]{:S(2)}) copy-start(bf16[416,32]{1,0:T(8,128)(2,1)} %constant.58.clone.rep_ref) | copy-start | bytes 79876
  151.7 19.5 %copy-start.8 = (bf16[32,224]{1,0:T(8,128)(2,1)S(1)}, bf16[32,224]{1,0:T(8,128)(2,1)}, u32[]{:S(2)}) copy-start(bf16[32,224]{1,0:T(8,128)(2,1)} %constant.59.clone.rept_ref) | copy-start | bytes 43012
  167.3 3.9 %copy-start.2 = (bf16[1280,4096]{1,0:T(8,128)(2,1)}, bf16[1280,4096]{1,0:T(8,128)(2,1)S(1)}, u32[]{:S(2)}) copy-start(bf16[1280,4096]{1,0:T(8,128)(2,1)S(1)} %tower_pairs.1.pg_ref) | copy-start | bytes 31457284
  198.3 27.3 %collective-permute-start.26 = (f32[208,128]{1,0:T(8,128)S(1)}, f32[208,128]{1,0:T(8,128)S(1)}, u32[]{:S(2)}, u32[]{:S(2)}) collective-permute-start(f32[208,128]{1,0:T(8,128)S(1)} %fusion.2), channel_id=1, source_target_pairs={{0,4},{4,0},{8,12},{12,8},{16,20},{20,16},{24,28},{28,24},{32,36},... | collective-permute-start | bytes 319496 | tf_op jit(solution)/shard_map/ppermute | solution.py:115
  198.4 94.5 %all-to-all-start.2 = ((bf16[32,416,128]{2,1,0:T(8,128)(2,1)}), bf16[32,416,128]{2,1,0:T(8,128)(2,1)}, u32[]{:S(2)}, u32[]{:S(2)}) async-start(bf16[32,416,128]{2,1,0:T(8,128)(2,1)} %get-tuple-element.18), calls=%async_computation.2 | async-start | bytes 6815744 | tf_op jit(solution)/shard_map/all_to_all | solution.py:547
  220.5 43.3 %collective-permute-start.13 = (bf16[1280,256]{1,0:T(8,128)(2,1)S(1)}, bf16[1280,256]{1,0:T(8,128)(2,1)S(1)}, u32[]{:S(2)}, u32[]{:S(2)}) collective-permute-start(bf16[1280,256]{1,0:T(8,128)(2,1)S(1)} %get-tuple-element.21), channel_id=1, source_target_pairs={{0,1},{1,0},{2,3},{3,2},{4,5},{5,4},{6,7},{7,6},{8,9},{9,8},{10,11... | collective-permute-start | bytes 1966088 | tf_op jit(solution)/shard_map/ppermute | solution.py:115
  224.1 40.3 %collective-permute-start.14 = (bf16[1280,256]{1,0:T(8,128)(2,1)S(1)}, bf16[1280,256]{1,0:T(8,128)(2,1)S(1)}, u32[]{:S(2)}, u32[]{:S(2)}) collective-permute-start(bf16[1280,256]{1,0:T(8,128)(2,1)S(1)} %get-tuple-element.22), channel_id=1, source_target_pairs={{0,2},{1,3},{2,0},{3,1},{4,6},{5,7},{6,4},{7,5},{8,10},{9,11},{10,... | collective-permute-start | bytes 1966088 | tf_op jit(solution)/shard_map/ppermute | solution.py:115
  224.1 40.3 %collective-permute-start.15 = (bf16[1280,256]{1,0:T(8,128)(2,1)S(1)}, bf16[1280,256]{1,0:T(8,128)(2,1)S(1)}, u32[]{:S(2)}, u32[]{:S(2)}) collective-permute-start(bf16[1280,256]{1,0:T(8,128)(2,1)S(1)} %get-tuple-element.23), channel_id=1, source_target_pairs={{0,3},{1,2},{2,1},{3,0},{4,7},{5,6},{6,5},{7,4},{8,11},{9,10},{10,... | collective-permute-start | bytes 1966088 | tf_op jit(solution)/shard_map/ppermute | solution.py:115
  225.7 30.4 %collective-permute-start.27 = (f32[208,128]{1,0:T(8,128)S(1)}, f32[208,128]{1,0:T(8,128)S(1)}, u32[]{:S(2)}, u32[]{:S(2)}) collective-permute-start(f32[208,128]{1,0:T(8,128)S(1)} %fusion.17), channel_id=1, source_target_pairs={{0,1},{1,0},{2,3},{3,2},{4,5},{5,4},{6,7},{7,6},{8,9},{9,8},{10,11... | collective-permute-start | bytes 319496 | tf_op jit(solution)/shard_map/ppermute | solution.py:115
  229.6 27.4 %collective-permute-start.28 = (f32[208,128]{1,0:T(8,128)S(1)}, f32[208,128]{1,0:T(8,128)S(1)}, u32[]{:S(2)}, u32[]{:S(2)}) collective-permute-start(f32[208,128]{1,0:T(8,128)S(1)} %fusion.17), channel_id=1, source_target_pairs={{0,2},{1,3},{2,0},{3,1},{4,6},{5,7},{6,4},{7,5},{8,10},{9,11},{10,... | collective-permute-start | bytes 319496 | tf_op jit(solution)/shard_map/ppermute | solution.py:115
  256.1 4.7 %collective-permute-start.29 = (f32[208,128]{1,0:T(8,128)S(1)}, f32[208,128]{1,0:T(8,128)S(1)}, u32[]{:S(2)}, u32[]{:S(2)}) collective-permute-start(f32[208,128]{1,0:T(8,128)S(1)} %fusion.17), channel_id=1, source_target_pairs={{0,3},{1,2},{2,1},{3,0},{4,7},{5,6},{6,5},{7,4},{8,11},{9,10},{10,... | collective-permute-start | bytes 319496 | tf_op jit(solution)/shard_map/ppermute | solution.py:115
  260.8 5.3 %collective-permute-start.30 = (f32[208,128]{1,0:T(8,128)S(1)}, f32[208,128]{1,0:T(8,128)S(1)}, u32[]{:S(2)}, u32[]{:S(2)}) collective-permute-start(f32[208,128]{1,0:T(8,128)S(1)} %add_add_fusion.1), channel_id=1, source_target_pairs={{0,8},{4,12},{8,0},{12,4},{16,24},{20,28},{24,16},{28,20},{32,40},... | collective-permute-start | bytes 319496 | tf_op jit(solution)/shard_map/ppermute | solution.py:115
  261.2 6.5 %collective-permute-start.31 = (f32[208,128]{1,0:T(8,128)S(1)}, f32[208,128]{1,0:T(8,128)S(1)}, u32[]{:S(2)}, u32[]{:S(2)}) collective-permute-start(f32[208,128]{1,0:T(8,128)S(1)} %add_add_fusion.1), channel_id=1, source_target_pairs={{0,16},{4,20},{8,24},{12,28},{16,0},{20,4},{24,8},{28,12},{32,48},... | collective-permute-start | bytes 319496 | tf_op jit(solution)/shard_map/ppermute | solution.py:115
  263.8 5.0 %collective-permute-start.32 = (f32[208,128]{1,0:T(8,128)S(1)}, f32[208,128]{1,0:T(8,128)S(1)}, u32[]{:S(2)}, u32[]{:S(2)}) collective-permute-start(f32[208,128]{1,0:T(8,128)S(1)} %add_add_fusion.1), channel_id=1, source_target_pairs={{0,24},{4,28},{8,16},{12,20},{16,8},{20,12},{24,0},{28,4},{32,56},... | collective-permute-start | bytes 319496 | tf_op jit(solution)/shard_map/ppermute | solution.py:115
  264.8 11.5 %collective-permute-start.16 = (bf16[160,256]{1,0:T(8,128)(2,1)S(1)}, bf16[160,256]{1,0:T(8,128)(2,1)S(1)}, u32[]{:S(2)}, u32[]{:S(2)}) collective-permute-start(bf16[160,256]{1,0:T(8,128)(2,1)S(1)} %get-tuple-element.65), channel_id=1, source_target_pairs={{0,4},{4,0},{8,12},{12,8},{16,20},{20,16},{24,28},{28,24},{32,36},... | collective-permute-start | bytes 245768 | tf_op jit(solution)/shard_map/ppermute | solution.py:115
  268.8 43.5 %collective-permute-start.33 = (f32[208,128]{1,0:T(8,128)S(1)}, f32[208,128]{1,0:T(8,128)S(1)}, u32[]{:S(2)}, u32[]{:S(2)}) collective-permute-start(f32[208,128]{1,0:T(8,128)S(1)} %add_add_fusion), channel_id=1, source_target_pairs={{0,32},{4,36},{8,40},{12,44},{16,48},{20,52},{24,56},{28,60},{32,0... | collective-permute-start | bytes 319496 | tf_op jit(solution)/shard_map/ppermute | solution.py:115
  270.4 43.4 %collective-permute-start.34 = (f32[208,128]{1,0:T(8,128)S(1)}, f32[208,128]{1,0:T(8,128)S(1)}, u32[]{:S(2)}, u32[]{:S(2)}) collective-permute-start(f32[208,128]{1,0:T(8,128)S(1)} %add_add_fusion), channel_id=1, source_target_pairs={{0,64},{4,68},{8,72},{12,76},{16,80},{20,84},{24,88},{28,92},{32,9... | collective-permute-start | bytes 319496 | tf_op jit(solution)/shard_map/ppermute | solution.py:115
  273.1 40.7 %collective-permute-start.35 = (f32[208,128]{1,0:T(8,128)S(1)}, f32[208,128]{1,0:T(8,128)}, u32[]{:S(2)}, u32[]{:S(2)}) collective-permute-start(f32[208,128]{1,0:T(8,128)S(1)} %add_add_fusion), channel_id=1, source_target_pairs={{0,96},{4,100},{8,104},{12,108},{16,112},{20,116},{24,120},{28,124... | collective-permute-start | bytes 319496 | tf_op jit(solution)/shard_map/ppermute | solution.py:115
  273.6 5.3 %collective-permute-start.17 = (bf16[160,256]{1,0:T(8,128)(2,1)S(1)}, bf16[160,256]{1,0:T(8,128)(2,1)S(1)}, u32[]{:S(2)}, u32[]{:S(2)}) collective-permute-start(bf16[160,256]{1,0:T(8,128)(2,1)S(1)} %get-tuple-element.64), channel_id=1, source_target_pairs={{0,8},{4,12},{8,0},{12,4},{16,24},{20,28},{24,16},{28,20},{32,40},... | collective-permute-start | bytes 245768 | tf_op jit(solution)/shard_map/ppermute | solution.py:115
  276.3 4.9 %collective-permute-start.18 = (bf16[160,256]{1,0:T(8,128)(2,1)S(1)}, bf16[160,256]{1,0:T(8,128)(2,1)S(1)}, u32[]{:S(2)}, u32[]{:S(2)}) collective-permute-start(bf16[160,256]{1,0:T(8,128)(2,1)S(1)} %get-tuple-element.63), channel_id=1, source_target_pairs={{0,12},{4,8},{8,4},{12,0},{16,28},{20,24},{24,20},{28,16},{32,44},... | collective-permute-start | bytes 245768 | tf_op jit(solution)/shard_map/ppermute | solution.py:115
  278.8 5.9 %collective-permute-start.19 = (bf16[160,256]{1,0:T(8,128)(2,1)S(1)}, bf16[160,256]{1,0:T(8,128)(2,1)S(1)}, u32[]{:S(2)}, u32[]{:S(2)}) collective-permute-start(bf16[160,256]{1,0:T(8,128)(2,1)S(1)} %get-tuple-element.62), channel_id=1, source_target_pairs={{0,16},{4,20},{8,24},{12,28},{16,0},{20,4},{24,8},{28,12},{32,48},... | collective-permute-start | bytes 245768 | tf_op jit(solution)/shard_map/ppermute | solution.py:115
  281.2 5.5 %collective-permute-start.20 = (bf16[160,256]{1,0:T(8,128)(2,1)S(1)}, bf16[160,256]{1,0:T(8,128)(2,1)S(1)}, u32[]{:S(2)}, u32[]{:S(2)}) collective-permute-start(bf16[160,256]{1,0:T(8,128)(2,1)S(1)} %get-tuple-element.61), channel_id=1, source_target_pairs={{0,20},{4,16},{8,28},{12,24},{16,4},{20,0},{24,12},{28,8},{32,52},... | collective-permute-start | bytes 245768 | tf_op jit(solution)/shard_map/ppermute | solution.py:115
  284.8 4.4 %collective-permute-start.21 = (bf16[160,256]{1,0:T(8,128)(2,1)S(1)}, bf16[160,256]{1,0:T(8,128)(2,1)S(1)}, u32[]{:S(2)}, u32[]{:S(2)}) collective-permute-start(bf16[160,256]{1,0:T(8,128)(2,1)S(1)} %get-tuple-element.60), channel_id=1, source_target_pairs={{0,24},{4,28},{8,16},{12,20},{16,8},{20,12},{24,0},{28,4},{32,56},... | collective-permute-start | bytes 245768 | tf_op jit(solution)/shard_map/ppermute | solution.py:115
  286.7 4.6 %collective-permute-start.22 = (bf16[160,256]{1,0:T(8,128)(2,1)S(1)}, bf16[160,256]{1,0:T(8,128)(2,1)S(1)}, u32[]{:S(2)}, u32[]{:S(2)}) collective-permute-start(bf16[160,256]{1,0:T(8,128)(2,1)S(1)} %get-tuple-element.59), channel_id=1, source_target_pairs={{0,28},{4,24},{8,20},{12,16},{16,12},{20,8},{24,4},{28,0},{32,60},... | collective-permute-start | bytes 245768 | tf_op jit(solution)/shard_map/ppermute | solution.py:115
  292.1 0.9 copy-start.5
  292.1 0.9 copy-start.6
  292.1 0.9 copy-start.9
  292.1 0.9 copy-start.11
  300.3 23.7 %all-to-all-start.3 = ((bf16[96,1,1,32,128]{4,3,2,1,0:T(8,128)(2,1)}), bf16[96,1,1,32,128]{4,3,2,1,0:T(8,128)(2,1)S(1)}, u32[]{:S(2)}, u32[]{:S(2)}) async-start(bf16[96,1,1,32,128]{4,3,2,1,0:T(8,128)(2,1)} %bitcast.47), calls=%async_computation.3 | async-start | bytes 1572864 | tf_op jit(solution)/shard_map/all_to_all | solution.py:570
  308.9 8.3 %collective-permute-start.23 = (bf16[282,256]{1,0:T(8,128)(2,1)S(1)}, bf16[282,256]{1,0:T(8,128)(2,1)S(1)}, u32[]{:S(2)}, u32[]{:S(2)}) collective-permute-start(bf16[282,256]{1,0:T(8,128)(2,1)S(1)} %get-tuple-element.76), channel_id=1, source_target_pairs={{0,1},{1,0},{2,3},{3,2},{4,5},{5,4},{6,7},{7,6},{8,9},{9,8},{10,11... | collective-permute-start | bytes 433160 | tf_op jit(solution)/shard_map/ppermute | solution.py:115
  312.2 7.4 %collective-permute-start.24 = (bf16[282,256]{1,0:T(8,128)(2,1)S(1)}, bf16[282,256]{1,0:T(8,128)(2,1)S(1)}, u32[]{:S(2)}, u32[]{:S(2)}) collective-permute-start(bf16[282,256]{1,0:T(8,128)(2,1)S(1)} %get-tuple-element.75), channel_id=1, source_target_pairs={{0,2},{1,3},{2,0},{3,1},{4,6},{5,7},{6,4},{7,5},{8,10},{9,11},{10,... | collective-permute-start | bytes 433160 | tf_op jit(solution)/shard_map/ppermute | solution.py:115
  312.3 8.7 %collective-permute-start.25 = (bf16[282,256]{1,0:T(8,128)(2,1)S(1)}, bf16[282,256]{1,0:T(8,128)(2,1)S(1)}, u32[]{:S(2)}, u32[]{:S(2)}) collective-permute-start(bf16[282,256]{1,0:T(8,128)(2,1)S(1)} %get-tuple-element.77), channel_id=1, source_target_pairs={{0,3},{1,2},{2,1},{3,0},{4,7},{5,6},{6,5},{7,4},{8,11},{9,10},{10,... | collective-permute-start | bytes 433160 | tf_op jit(solution)/shard_map/ppermute | solution.py:115
  322.8 2.2 copy-start.1
Sparse Core Ops, SparseCore 0:
  10.2 111.0 all-gather.1
